TPU v7x, 128 devices: a whole 4x4x4 slice. The times are simulated.
128 devices in a mesh: lat: 8 (over z, core), lon: 16 (over x, y).
Axes of the slice: x: 4, y: 4, z: 4, core: 2. Of those that a mesh axis runs over, the one named last changes fastest.
Arguments:
- grid_nodes: bfloat16 [131072, 512], P(('lat', 'lon')), may hold values from -6 to 6
- grid_edges: bfloat16 [36864, 512], P(('lat', 'lon')), may hold values from -6 to 6
- grid_sender: int32 [36864], P(('lat', 'lon')), may hold values from 0 to 1023
- owner_index: int32 [36864], P(('lat', 'lon')), may hold values from -1 to 255, as said below
- mesh_nodes: bfloat16 [32768, 512], P(('lat', 'lon')), may hold values from -6 to 6
- mesh_edges: bfloat16 [65536, 512], P(('lat', 'lon')), may hold values from -6 to 6
- mesh_sender: int32 [65536], P(('lat', 'lon')), may hold values from 0 to 1023
- mesh_receiver: int32 [65536], P(('lat', 'lon')), may hold values from 0 to 255
- w_first: bfloat16 [3, 1536, 512], replicated, may hold values from -0.15625 to 0.15625
- first_bias: float32 [3, 512], replicated, may hold values from -3 to 3
- w_second: bfloat16 [3, 512, 512], replicated, may hold values from -0.25 to 0.25
- norm_gain: float32 [3, 512], replicated, may hold values from 0.25 to 1.75
- mesh_cotangent: bfloat16 [32768, 512], P(('lat', 'lon')), may hold values from -0.01953125 to 0.01953125
- edge_cotangent: bfloat16 [65536, 512], P(('lat', 'lon')), may hold values from -0.01953125 to 0.01953125
Outputs:
- updated_mesh: bfloat16 [32768, 512], P(('lat', 'lon'))
- updated_edges: bfloat16 [65536, 512], P(('lat', 'lon'))
- grad_first: float32 [3, 1536, 512], P(None, 'lat', 'lon')
- grad_second: float32 [3, 512, 512], P(None, 'lat', 'lon')
Inputs may be any that keep to these rules, and one draw needn't show every extreme that they name: `owner_index`: The used slots of a block come first. Blocks from beyond the first or last latitude band are unused. Some device receives 32 used slots from every device that sends to it.
All inputs are finite; a program needn't handle non-finite values.
Results may differ from a plain program's by a relative error of at most 0.02.
Values may be sent and summed in bfloat16 or wider, within the bound.
No kernel may reach another device: no remote copies, remote signals or barrier semaphores. Data moves between devices by JAX's collectives and lax.ppermute only.
A program may use at most 128 MiB of HBM per device.

v0:
```python
import jax
import jax.numpy as jnp
from jax import lax
from jax.experimental import pallas as pl
from jax.experimental.pallas import tpu as pltpu
from jax.sharding import Mesh
from jax.sharding import PartitionSpec as P

D = 512
CAP = 32
BORDER = 64
K_COARSE = 4
EPSILON = 1e-05
ALL = ("z", "c", "x", "y")
LAT = ("z", "c")
LON = ("x", "y")
F32 = jnp.float32
BF16 = jnp.bfloat16


SLOT_ROWS = 2 * CAP
PACKET = 3 * SLOT_ROWS + BORDER


def lon_pairs(by, lats, lons):
    return [
        (lat * lons + lon, lat * lons + (lon + by) % lons)
        for lat in range(lats)
        for lon in range(lons)
    ]


def chip_pairs(lats, lons):
    pairs = []
    for lat in range(1, lats - 1, 2):
        for lon in range(lons):
            lower, upper = lat * lons + lon, (lat + 1) * lons + lon
            pairs += [(lower, upper), (upper, lower)]
    return pairs


def in_hbm(arrays):
    return [pltpu.with_memory_space_constraint(a, pltpu.HBM) for a in arrays]


def dot(a, b):
    return jnp.dot(a, b, preferred_element_type=F32)


def dot_nt(a, b):
    return lax.dot_general(a, b, (((1,), (1,)), ((), ())), preferred_element_type=F32)


def dot_tn(a, b):
    return lax.dot_general(a, b, (((0,), (0,)), ((), ())), preferred_element_type=F32)


def down_onehot(index, count):
    index = index.reshape(1, -1)
    lines = lax.broadcasted_iota(jnp.int32, (count, index.shape[1]), 0)
    return jnp.where(lines == index, 1.0, 0.0).astype(BF16)


def coarse_line(row):
    at = row - 512
    device = at >> 2
    chip = ((device >> 5) << 4) + (device & 15)
    other = ((device >> 4) & 1) ^ lax.axis_index("c")
    return jnp.where(at < 0, -2 * K_COARSE, other * 512 + chip * 8 + (at & 3))


def pack_kernel(*refs):
    hbm, (east, west, middle, coarse), (picked, sem), local = (
        refs[:4],
        refs[4:8],
        refs[8:10],
        refs[10:],
    )
    loads = [
        pltpu.make_async_copy(source, to, sem.at[i])
        for i, (source, to) in enumerate(zip(hbm, local))
    ]
    for load in loads:
        load.start()
    for load in loads:
        load.wait()
    points, slot_edges, senders, nodes = local
    picked[...] = dot_tn(down_onehot(senders[...], points.shape[0]), points[...]).astype(BF16)
    toward_core = jnp.where(lax.axis_index("c") == 1, 0, 2)
    bands = (1, toward_core, 2 - toward_core)
    for column, out in ((2, east), (0, west), (1, middle)):
        for at, band in enumerate(bands):
            block = pl.multiple_of((band * 3 + column) * CAP, CAP)
            to = at * SLOT_ROWS
            out[to : to + CAP, :] = slot_edges[pl.ds(block, CAP), :]
            out[to + CAP : to + SLOT_ROWS, :] = picked[pl.ds(block, CAP), :]
        out[3 * SLOT_ROWS : PACKET, :] = nodes[0:BORDER, :]
    rows = nodes[nodes.shape[0] - 8 :, :].astype(F32)[8 - K_COARSE :, :]
    halves = jnp.concatenate([rows[:, : D // 2], rows[:, D // 2 :]], axis=0).astype(BF16)
    coarse[...] = jnp.broadcast_to(halves[None], coarse.shape)


def packets(points, slot_edges, senders, nodes):
    packet = jax.ShapeDtypeStruct((PACKET, D), BF16)
    vmem = pl.BlockSpec(memory_space=pltpu.VMEM)
    return pl.pallas_call(
        pack_kernel,
        out_shape=[packet] * 3 + [jax.ShapeDtypeStruct((64, 2 * K_COARSE, D // 2), BF16)],
        in_specs=[pl.BlockSpec(memory_space=pltpu.HBM)] * 4,
        out_specs=[vmem] * 4,
        scratch_shapes=[pltpu.VMEM((9 * CAP, D), BF16), pltpu.SemaphoreType.DMA((4,))]
        + [pltpu.VMEM(a.shape, a.dtype) for a in (points, slot_edges, senders, nodes)],
        name="pack",
        compiler_params=pltpu.CompilerParams(vmem_limit_bytes=16 << 20),
        cost_estimate=pl.CostEstimate(
            flops=2 * 288 * 1024 * 512, bytes_accessed=2 << 20, transcendentals=0
        ),
    )(*in_hbm((points, slot_edges, senders, nodes)))


def relay_kernel(from_west, from_east, middle, to_core, to_chip):
    for at, out in ((1, to_core), (2, to_chip)):
        rows = slice(at * SLOT_ROWS, (at + 1) * SLOT_ROWS)
        for i, source in enumerate((from_west, middle, from_east)):
            out[i * SLOT_ROWS : (i + 1) * SLOT_ROWS, :] = source[rows, :]
        out[3 * SLOT_ROWS : PACKET, :] = middle[3 * SLOT_ROWS : PACKET, :]


def relay(from_west, from_east, middle):
    vmem = pl.BlockSpec(memory_space=pltpu.VMEM)
    return pl.pallas_call(
        relay_kernel,
        out_shape=[jax.ShapeDtypeStruct((PACKET, D), BF16)] * 2,
        in_specs=[vmem] * 3,
        out_specs=[vmem] * 2,
        name="relay",
        compiler_params=pltpu.CompilerParams(vmem_limit_bytes=16 << 20),
        cost_estimate=pl.CostEstimate(flops=10**6, bytes_accessed=1 << 20, transcendentals=0),
    )(from_west, from_east, middle)


def forward(pre, w_second, gain, slope, hid, norm, scale):
    sig = 0.5 + 0.5 * jnp.tanh(0.5 * pre)
    act = pre * sig
    hid[...] = act.astype(BF16)
    slope[...] = sig + act * (1.0 - sig)
    out = dot(hid[...], w_second)
    out = out - jnp.mean(out, axis=1, keepdims=True)
    size = lax.rsqrt(jnp.mean(out * out, axis=1, keepdims=True) + EPSILON)
    scale[...] = jnp.broadcast_to(size, scale.shape)
    unit = out * size
    norm[...] = unit
    return unit * gain


def backward(dy, w_second, gain, slope, norm, scale):
    unit = norm[...]
    dn = dy * gain
    mid = jnp.mean(dn, axis=1, keepdims=True)
    along = jnp.mean(dn * unit, axis=1, keepdims=True)
    d_out = (scale[:, 0:1] * (dn - mid - unit * along)).astype(BF16)
    d_hid = dot_nt(d_out, w_second).astype(BF16)
    d_pre = (d_hid.astype(F32) * slope[...]).astype(BF16)
    return d_pre, d_out


def weight_grads(x, hid, d_pre, d_out, keep, send):
    odd = lax.axis_index("c") == 1
    low = lax.broadcasted_iota(jnp.int32, (D, 128), 1) < 64
    second = dot_tn(d_out, hid[...])
    for z in range(4):
        first = dot_tn(d_pre, x[:, 384 * z : 384 * (z + 1)])
        turned = pltpu.roll(second[:, 128 * z : 128 * (z + 1)], 64, 1)
        middle = first[:, 128:256]
        even_a, odd_a = first[:, 0:128], first[:, 256:384]
        even_b = jnp.where(low, middle, turned)
        odd_b = jnp.where(low, turned, middle)
        for ref, a, b in (
            (keep, jnp.where(odd, odd_a, even_a), jnp.where(odd, odd_b, even_b)),
            (send, jnp.where(odd, even_a, odd_a), jnp.where(odd, even_b, odd_b)),
        ):
            ref[16 * z : 16 * (z + 1), :, 0:128] = a.astype(BF16).reshape(16, 32, 128)
            ref[16 * z : 16 * (z + 1), :, 128:256] = b.astype(BF16).reshape(16, 32, 128)


LOADED = (
    "edge_receiver",
    "mesh_sender",
    "nodes",
    "w_first",
    "edges",
    "first_bias",
    "owner",
    "norm_gain",
    "w_second",
    "mesh_cot",
    "edge_cot",
)


def local_kernel(from_west, from_east, coarse_own, coarse_other, *refs):
    n = len(LOADED)
    hbm, vmem = refs[:n], refs[n : 2 * n]
    middle, received, pre, sem, table = refs[2 * n :]
    to = dict(zip(LOADED, vmem))
    loads = {
        name: pltpu.make_async_copy(source, target, sem.at[i])
        for i, (name, source, target) in enumerate(zip(LOADED, hbm, vmem))
        if name != "w_first"
    }
    w_first = dict(zip(LOADED, hbm))["w_first"]
    for k in range(3):
        loads[f"w_first_{k}"] = pltpu.make_async_copy(
            w_first.at[k], to["w_first"].at[k], sem.at[n + k]
        )
    for name in ("edge_receiver", "mesh_sender", "nodes", "w_first_1", "edges", "first_bias"):
        loads[name].start()
    rest = [name for name in loads if name in ("owner", "norm_gain", "w_second", "mesh_cot", "edge_cot")]
    rest += ["w_first_0", "w_first_2"]
    for name in rest:
        loads[name].start()
    for name in ("edge_receiver", "mesh_sender", "nodes"):
        loads[name].wait()
    nodes = to["nodes"]
    n_nodes = nodes.shape[0]
    table[0:n_nodes, :] = nodes[...]
    table[n_nodes : n_nodes + BORDER, :] = from_west[3 * SLOT_ROWS :, :]
    table[n_nodes + BORDER :, :] = from_east[3 * SLOT_ROWS :, :]
    sender = to["mesh_sender"][...]
    line = jnp.where(sender < n_nodes, sender, jnp.where(sender < n_nodes + 2 * BORDER, -1, sender - 2 * BORDER))
    near = dot_tn(down_onehot(line, table.shape[0]), table[...])
    line = coarse_line(sender)
    halves = coarse_own.shape[0]
    for half in range(2):
        hot = down_onehot(line + half * K_COARSE, 2 * halves)
        part = dot_tn(hot[:halves], coarse_own[...]) + dot_tn(hot[halves:], coarse_other[...])
        columns = slice(256 * half, 256 * (half + 1))
        middle[:, columns] = (near[:, columns] + part).astype(BF16)
    received[...] = dot_tn(down_onehot(to["edge_receiver"][...], n_nodes), nodes[...]).astype(BF16)
    for name in ("w_first_1", "edges", "first_bias"):
        loads[name].wait()
    w = to["w_first"]
    pre[...] = (
        dot(to["edges"][...], w[1, 0:D, :])
        + dot(received[...], w[1, 2 * D :, :])
        + to["first_bias"][1:2, :]
    )
    for name in rest:
        loads[name].wait()


def local(near, loaded):
    vmem = pl.BlockSpec(memory_space=pltpu.VMEM)
    hbm = pl.BlockSpec(memory_space=pltpu.HBM)
    out = pl.pallas_call(
        local_kernel,
        out_shape=[jax.ShapeDtypeStruct(a.shape, a.dtype) for a in loaded]
        + [
            jax.ShapeDtypeStruct((512, D), BF16),
            jax.ShapeDtypeStruct((512, D), BF16),
            jax.ShapeDtypeStruct((512, D), F32),
        ],
        in_specs=[vmem] * len(near) + [hbm] * len(loaded),
        out_specs=[vmem] * (len(loaded) + 3),
        scratch_shapes=[
            pltpu.SemaphoreType.DMA((len(loaded) + 3,)),
            pltpu.VMEM((256 + 2 * BORDER, D), BF16),
        ],
        name="local",
        compiler_params=pltpu.CompilerParams(vmem_limit_bytes=26 << 20),
        cost_estimate=pl.CostEstimate(
            flops=2 * 10**9, bytes_accessed=10 << 20, transcendentals=0
        ),
    )(*near, *in_hbm(loaded))
    return dict(zip(LOADED + ("middle", "received", "pre"), out))


def kept_shapes(rows):
    return [
        ((rows, 3 * D), BF16),
        ((rows, D), BF16),
        ((rows, D), F32),
        ((rows, D), F32),
        ((rows, 128), F32),
        ((256, D), BF16),
    ]


CHUNKS = ((64, 32, 256), BF16)


def nodes_kernel(
    from_west,
    from_east,
    centre,
    from_core,
    from_chip,
    owner,
    edge_sender,
    edge_receiver,
    nodes,
    edges,
    w_first,
    first_bias,
    w_second,
    norm_gain,
    mesh_cot,
    middle,
    received,
    pre_edge,
    updated_mesh_out,
    updated_edges_out,
    keep,
    send,
    x_edge,
    hid_edge,
    slope_edge,
    norm_edge,
    scale_edge,
    d_edge,
    x_grid,
    hid_grid,
    slope_grid,
    norm_grid,
    scale_grid,
    d_grid,
    x_node,
    hid_node,
    slope_node,
    norm_node,
    scale_node,
    updated_mesh,
    updated_edges,
    borders,
    sem,
):
    store_mesh = pltpu.make_async_copy(updated_mesh, updated_mesh_out, sem.at[0])
    store_edges = pltpu.make_async_copy(updated_edges, updated_edges_out, sem.at[1])
    n_nodes = nodes.shape[0]
    odd = lax.axis_index("c") == 1
    lower = jnp.where(odd, from_core[...], from_chip[...])
    upper = jnp.where(odd, from_chip[...], from_core[...])
    same = (from_west[0:SLOT_ROWS, :], centre[0:SLOT_ROWS, :], from_east[0:SLOT_ROWS, :])
    for block in range(9):
        rows = slice(block * CAP, (block + 1) * CAP)
        at = block % 3
        if block // 3 == 1:
            packet = same[at]
        else:
            packet = (lower, None, upper)[block // 3][at * SLOT_ROWS : (at + 1) * SLOT_ROWS, :]
        x_grid[rows, 0:D] = packet[0:CAP, :]
        x_grid[rows, D : 2 * D] = packet[CAP:SLOT_ROWS, :]
    borders[0:BORDER, :] = lower[3 * SLOT_ROWS :, :]
    borders[BORDER:, :] = upper[3 * SLOT_ROWS :, :]

    bordering = dot_tn(down_onehot(edge_sender[...] - n_nodes, 2 * BORDER), borders[...])
    x_edge[:, 0:D] = edges[...]
    x_edge[:, D : 2 * D] = (middle[...].astype(F32) + bordering).astype(BF16)
    x_edge[:, 2 * D :] = received[...]
    pre = pre_edge[...] + dot(x_edge[:, D : 2 * D], w_first[1, D : 2 * D, :])
    y_edge = forward(
        pre, w_second[1], norm_gain[1:2, :], slope_edge, hid_edge, norm_edge, scale_edge
    )
    updated_edges[...] = (edges[...].astype(F32) + y_edge).astype(BF16)
    store_edges.start()
    x_node[:, 2 * D :] = dot(
        down_onehot(edge_receiver[...], n_nodes), y_edge.astype(BF16)
    ).astype(BF16)

    owner_hot = down_onehot(owner[...], n_nodes)
    x_grid[:, 2 * D :] = dot_tn(owner_hot, nodes[...]).astype(BF16)
    pre = dot(x_grid[...], w_first[0]) + first_bias[0:1, :]
    y_grid = forward(
        pre, w_second[0], norm_gain[0:1, :], slope_grid, hid_grid, norm_grid, scale_grid
    )
    x_node[:, D : 2 * D] = dot(owner_hot, y_grid.astype(BF16)).astype(BF16)

    x_node[:, 0:D] = nodes[...]
    pre = dot(x_node[...], w_first[2]) + first_bias[2:3, :]
    gain = norm_gain[2:3, :]
    y_node = forward(pre, w_second[2], gain, slope_node, hid_node, norm_node, scale_node)
    updated_mesh[...] = (nodes[...].astype(F32) + y_node).astype(BF16)
    store_mesh.start()
    d_pre, d_out = backward(
        mesh_cot[...].astype(F32), w_second[2], gain, slope_node, norm_node, scale_node
    )
    d_grid[...] = dot_nt(d_pre, w_first[2, D : 2 * D, :]).astype(BF16)
    d_edge[...] = dot_nt(d_pre, w_first[2, 2 * D :, :]).astype(BF16)
    weight_grads(x_node, hid_node, d_pre, d_out, keep, send)
    store_edges.wait()
    store_mesh.wait()


def node_pass(*args):
    vmem = pl.BlockSpec(memory_space=pltpu.VMEM)
    hbm = pl.BlockSpec(memory_space=pltpu.HBM)
    outs = [CHUNKS, CHUNKS] + kept_shapes(512) + kept_shapes(288)
    return pl.pallas_call(
        nodes_kernel,
        out_shape=[
            jax.ShapeDtypeStruct((256, D), BF16),
            jax.ShapeDtypeStruct((512, D), BF16),
        ]
        + [jax.ShapeDtypeStruct(*shape) for shape in outs],
        in_specs=[vmem] * len(args),
        out_specs=[hbm, hbm] + [vmem] * len(outs),
        scratch_shapes=[pltpu.VMEM(*shape) for shape in kept_shapes(256)[:5]]
        + [
            pltpu.VMEM((256, D), BF16),
            pltpu.VMEM((512, D), BF16),
            pltpu.VMEM((2 * BORDER, D), BF16),
            pltpu.SemaphoreType.DMA((2,)),
        ],
        name="node_pass",
        compiler_params=pltpu.CompilerParams(vmem_limit_bytes=22 << 20),
        cost_estimate=pl.CostEstimate(
            flops=4 * 10**9, bytes_accessed=20 << 20, transcendentals=10**6
        ),
    )(*args)


def edge_pass(k, index, cotangent, w_second, norm_gain, kept):
    given = () if cotangent is None else (cotangent,)

    def kernel(index, w_second, norm_gain, x, hid, slope, norm, scale, d_sum, *refs):
        keep, send = refs[-2:]
        dy = dot_tn(down_onehot(index[...], d_sum.shape[0]), d_sum[...])
        if given:
            dy = refs[0][...].astype(F32) + dy
        d_pre, d_out = backward(dy, w_second[k], norm_gain[k : k + 1, :], slope, norm, scale)
        weight_grads(x, hid, d_pre, d_out, keep, send)

    vmem = pl.BlockSpec(memory_space=pltpu.VMEM)
    args = (index, w_second, norm_gain, *kept, *given)
    return pl.pallas_call(
        kernel,
        out_shape=[jax.ShapeDtypeStruct(*CHUNKS)] * 2,
        in_specs=[vmem] * len(args),
        out_specs=[vmem] * 2,
        compiler_params=pltpu.CompilerParams(vmem_limit_bytes=24 << 20),
        cost_estimate=pl.CostEstimate(
            flops=2 * 10**9, bytes_accessed=8 << 20, transcendentals=10**4
        ),
    )(*args)


def this_place():
    return [lax.axis_index(axis) for axis in ("c", "z", "x", "y")]


def small_call(kernel, shapes, *args):
    vmem = pl.BlockSpec(memory_space=pltpu.VMEM)
    moved = sum(a.size * 2 for a in args)
    return pl.pallas_call(
        kernel,
        out_shape=[jax.ShapeDtypeStruct(shape, dtype) for shape, dtype in shapes],
        in_specs=[vmem] * len(args),
        out_specs=[vmem] * len(shapes),
        compiler_params=pltpu.CompilerParams(vmem_limit_bytes=12 << 20),
        cost_estimate=pl.CostEstimate(flops=moved, bytes_accessed=moved, transcendentals=0),
    )(*args)


Z, X, Y = 1, 2, 3
AXES = {0: (Y, X, Z), 1: (X, Z, Y), 2: (Z, Y, X)}


def masks(place):
    return 1 + 2 * place[0], 3 - 2 * place[0]


def partner_pairs(axis, second):
    pairs = []
    for device in range(128):
        z, c, x, y = device >> 5, (device >> 4) & 1, (device >> 2) & 3, device & 3
        mask = (3 - 2 * c) if second else (1 + 2 * c)
        at = {Z: z, X: x, Y: y}
        at[axis] ^= mask
        pairs.append((device, ((at[Z] * 2 + c) * 4 + at[X]) * 4 + at[Y]))
    return pairs


def swap_along(value, axis, second):
    return lax.ppermute(value, ALL, partner_pairs(axis, second))


def chunk_at(left, axis, i, r):
    n = len(left)
    stride = 4 ** (n - 1 - left.index(axis))
    low = r & (stride - 1)
    return (r - low) * 4 + i * stride + low


def halve(k, step, *inputs):
    axis = AXES[k][step]
    left = sorted(AXES[k][step:])
    count = 4 ** (len(left) - 1)

    def kernel(a, b, kept, sent):
        place = this_place()
        m1, m2 = masks(place)
        mine = place[axis]
        for out, base in ((kept, mine), (sent, mine ^ m1)):
            for j in range(2):
                i = base ^ (m2 * j)

                def body(r, carry):
                    at = chunk_at(left, axis, i, r)
                    out[j, r] = a[at] + b[at]
                    return carry

                lax.fori_loop(0, count, body, 0, unroll=min(count, 8))

    half = ((2, count, 32, 256), BF16)
    return small_call(kernel, (half, half), *inputs)


def quarter(kept, got):
    count = kept.shape[1]

    def kernel(kept, got, keep, send):
        for j, out in ((0, keep), (1, send)):

            def body(r, carry):
                out[r] = kept[j, r] + got[j, r]
                return carry

            lax.fori_loop(0, count, body, 0, unroll=min(count, 8))

    half = ((count, 32, 256), BF16)
    return small_call(kernel, (half, half), kept, got)


def reduced(k, keep, got):
    for step, axis in enumerate(AXES[k]):
        keep, send = halve(k, step, keep, got)
        got = swap_along(send, axis, False)
        keep, send = quarter(keep, got)
        got = swap_along(send, axis, True)
    return keep, got


def finish(terms):
    def kernel(*refs):
        grad_first, grad_second = refs[6:]
        odd = lax.axis_index("c") == 1
        for k in range(3):
            total = refs[2 * k][0].astype(F32) + refs[2 * k + 1][0].astype(F32)
            turned = pltpu.roll(total, 64, 1)
            grad_first[k] = jnp.where(odd, turned, total)[:, 0:192]
            grad_second[k] = jnp.where(odd, total[:, 128:192], turned[:, 0:64])

    shapes = (((3, 32, 192), F32), ((3, 32, 64), F32))
    return small_call(kernel, shapes, *[t for pair in terms for t in pair])


def shards(
    grid_nodes,
    grid_edges,
    grid_sender,
    owner_index,
    mesh_nodes,
    mesh_edges,
    mesh_sender,
    mesh_receiver,
    w_first,
    first_bias,
    w_second,
    norm_gain,
    mesh_cotangent,
    edge_cotangent,
):
    lats = lax.axis_size(LAT)
    lons = lax.axis_size(LON)
    swap = [(0, 1), (1, 0)]
    east, west, middle, coarse = packets(grid_nodes, grid_edges, grid_sender, mesh_nodes)
    from_west = lax.ppermute(east, ALL, lon_pairs(1, lats, lons))
    from_east = lax.ppermute(west, ALL, lon_pairs(-1, lats, lons))
    coarse_own = lax.all_to_all(coarse, ("z", "x", "y"), 0, 0, tiled=True)
    coarse_own = coarse_own.reshape(-1, D // 2)
    to_core, to_chip = relay(from_west, from_east, middle)
    from_chip = lax.ppermute(to_chip, ALL, chip_pairs(lats, lons))
    from_core = lax.ppermute(to_core, "c", swap)
    coarse_other = lax.ppermute(coarse_own, "c", swap)
    at = local(
        (from_west, from_east, coarse_own, coarse_other),
        (
            mesh_receiver,
            mesh_sender,
            mesh_nodes,
            w_first,
            mesh_edges,
            first_bias,
            owner_index,
            norm_gain,
            w_second,
            mesh_cotangent,
            edge_cotangent,
        ),
    )
    updated_mesh, updated_edges, keep, send, *kept = node_pass(
        from_west,
        from_east,
        middle,
        from_core,
        from_chip,
        at["owner"],
        at["mesh_sender"],
        at["edge_receiver"],
        at["nodes"],
        at["edges"],
        at["w_first"],
        at["first_bias"],
        at["w_second"],
        at["norm_gain"],
        at["mesh_cot"],
        at["middle"],
        at["received"],
        at["pre"],
    )
    terms = {2: reduced(2, keep, lax.ppermute(send, "c", swap))}
    for k, index, cotangent, saved in (
        (1, at["edge_receiver"], at["edge_cot"], kept[:6]),
        (0, at["owner"], None, kept[6:]),
    ):
        keep, send = edge_pass(k, index, cotangent, at["w_second"], at["norm_gain"], saved)
        terms[k] = reduced(k, keep, lax.ppermute(send, "c", swap))
    first, second = finish([terms[k] for k in range(3)])
    return (updated_mesh, updated_edges, first.transpose(0, 2, 1), second.transpose(0, 2, 1))


def solution(mesh):
    finer = Mesh(mesh.devices.reshape(4, 2, 4, 4), ALL)
    by_device = P(ALL, None)
    index = P(ALL)

    return jax.shard_map(
        shards,
        mesh=finer,
        in_specs=(
            by_device,
            by_device,
            index,
            index,
            by_device,
            by_device,
            index,
            index,
            P(),
            P(),
            P(),
            P(),
            by_device,
            by_device,
        ),
        out_specs=(by_device, by_device, P(None, LAT, LON), P(None, LAT, LON)),
        check_vma=False,
    )
```

profile of v0, /device:TPU:0, one launch (start us, length us, event | category | flops | bytes accessed | tf_op | source)
XLA Modules:
  0.0 91.1 jit_solution(15416223119001941549)
XLA Ops:
  0.6 2.5 %pack.1 = (bf16[256,512]{1,0:T(8,128)(2,1)S(1)}, bf16[256,512]{1,0:T(8,128)(2,1)S(1)}, bf16[256,512]{1,0:T(8,128)(2,1)S(1)}, bf16[64,8,256]{2,1,0:T(8,128)(2,1)}) custom-call(bf16[1024,512]{1,0:T(8,128)(2,1)} %refs_0_.2, bf16[288,512]{1,0:T(8,128)(2,1)} %refs_1_.2, s32[288]{0:T(512)} %refs_2_.2, bf16[256,512]{1,0:T(8,128)(2,1)} %refs_2_.3), custom_call_target="tpu_custom_call" | custom-call | flops 301989888 | bytes 2097152 | tf_op jit(solution)/shard_map/pack/pallas_call | solution.py:106
  3.1 11.5 %all-to-all-start = ((bf16[64,8,256]{2,1,0:T(8,128)(2,1)}), bf16[64,8,256]{2,1,0:T(8,128)(2,1)S(1)}, u32[]{:S(2)}, u32[]{:S(2)}) async-start(bf16[64,8,256]{2,1,0:T(8,128)(2,1)} %get-tuple-element.87), calls=%async_computation | async-start | bytes 524288 | tf_op jit(solution)/shard_map/all_to_all | solution.py:579
  14.6 1.6 %collective-permute-start = (bf16[256,512]{1,0:T(8,128)(2,1)S(1)}, bf16[256,512]{1,0:T(8,128)(2,1)S(1)}, u32[]{:S(2)}, u32[]{:S(2)}) collective-permute-start(bf16[256,512]{1,0:T(8,128)(2,1)S(1)} %get-tuple-element.82), channel_id=1, source_target_pairs={{0,1},{1,2},{2,3},{3,4},{4,5},{5,6},{6,7},{7,8},{8,9},{9,10},{10,1... | collective-permute-start | bytes 786440 | tf_op jit(solution)/shard_map/ppermute | solution.py:577
  16.3 3.8 %collective-permute-start.1 = (bf16[256,512]{1,0:T(8,128)(2,1)S(1)}, bf16[256,512]{1,0:T(8,128)(2,1)S(1)}, u32[]{:S(2)}, u32[]{:S(2)}) collective-permute-start(bf16[256,512]{1,0:T(8,128)(2,1)S(1)} %get-tuple-element.83), channel_id=1, source_target_pairs={{0,15},{1,0},{2,1},{3,2},{4,3},{5,4},{6,5},{7,6},{8,7},{9,8},{10,9... | collective-permute-start | bytes 786440 | tf_op jit(solution)/shard_map/ppermute | solution.py:578
  20.1 6.0 %all-to-all-done = bf16[64,8,256]{2,1,0:T(8,128)(2,1)S(1)} async-done(((bf16[64,8,256]{2,1,0:T(8,128)(2,1)}), bf16[64,8,256]{2,1,0:T(8,128)(2,1)S(1)}, u32[]{:S(2)}, u32[]{:S(2)}) %all-to-all-start) | async-done | bytes 262176 | tf_op jit(solution)/shard_map/all_to_all | solution.py:579
  26.1 0.0 collective-permute-start.4
  26.1 1.9 %collective-permute-done.from_west = bf16[256,512]{1,0:T(8,128)(2,1)S(1)} collective-permute-done((bf16[256,512]{1,0:T(8,128)(2,1)S(1)}, bf16[256,512]{1,0:T(8,128)(2,1)S(1)}, u32[]{:S(2)}, u32[]{:S(2)}) %collective-permute-start) | collective-permute-done | bytes 262176 | tf_op jit(solution)/shard_map/ppermute | solution.py:577
  27.9 0.0 collective-permute-done.1.from_east
  28.0 0.1 collective-permute-start.2
  28.1 0.7 collective-permute-start.3
  28.8 0.0 collective-permute-done.4.coarse_other
  28.8 3.5 %local.1 = (s32[512]{0:T(512)S(1)}, s32[512]{0:T(512)S(1)}, bf16[256,512]{1,0:T(8,128)(2,1)S(1)}, bf16[3,1536,512]{2,1,0:T(8,128)(2,1)S(1)}, bf16[512,512]{1,0:T...) custom-call(bf16[256,512]{1,0:T(8,128)(2,1)S(1)} %collective-permute, ...), custom_call_target="tpu_custom_call" | custom-call | flops 2000000000 | bytes 10485760 | tf_op jit(solution)/shard_map/local/pallas_call | solution.py:255
  32.3 0.0 collective-permute-done.2.from_core
  32.3 0.0 collective-permute-done.3.from_chip
  32.3 5.7 %node_pass.1 = (bf16[256,512]{1,0:T(8,128)(2,1)}, bf16[512,512]{1,0:T(8,128)(2,1)}, bf16[64,32,256]{2,1,0:T(8,128)(2,1)S(1)}, bf16[64,32,256]{2,1,0:T(8,128)(2,1...) custom-call(bf16[256,512]{1,0:T(8,128)(2,1)S(1)} %collective-permute, ...), custom_call_target="tpu_custom_call" | custom-call | flops 4000000000 | bytes 20971520 | tf_op jit(solution)/shard_map/node_pass/pallas_call | solution.py:398
  38.0 4.0 %collective-permute-start.19 = (bf16[64,32,256]{2,1,0:T(8,128)(2,1)S(1)}, bf16[64,32,256]{2,1,0:T(8,128)(2,1)S(1)}, u32[]{:S(2)}, u32[]{:S(2)}) collective-permute-start(bf16[64,32,256]{2,1,0:T(8,128)(2,1)S(1)} %get-tuple-element.145), channel_id=1, source_target_pairs={{0,16},{16,0},{1,17},{17,1},{2,18},{18,2},{3,19},{19,3},{4,20},{20... | collective-permute-start | bytes 3145736 | tf_op jit(solution)/shard_map/ppermute | solution.py:621
  42.0 2.5 %shard_map.172 = (bf16[64,32,256]{2,1,0:T(8,128)(2,1)S(1)}, bf16[64,32,256]{2,1,0:T(8,128)(2,1)S(1)}) custom-call(s32[512]{0:T(512)S(1)} %get-tuple-element.90.edge_receiver.index, bf16[3,512,512]{2,1,0:T(8,128)(2,1)S(1)} %get-tuple-element.95.w_second, f32[3,512]{1,0:T(4,128)S(1)} %get-tuple-element.96.norm_gain, ...), custom_call_target="tpu_custom_call" | custom-call | flops 2000000000 | bytes 8388608 | tf_op jit(solution)/shard_map/pallas_call | solution.py:435
  44.5 0.3 collective-permute-start.12
  44.7 1.9 %shard_map.165 = (bf16[64,32,256]{2,1,0:T(8,128)(2,1)S(1)}, bf16[64,32,256]{2,1,0:T(8,128)(2,1)S(1)}) custom-call(s32[288]{0:T(512)S(1)} %get-tuple-element.88.owner.index, bf16[3,512,512]{2,1,0:T(8,128)(2,1)S(1)} %get-tuple-element.95.w_second, f32[3,512]{1,0:T(4,128)S(1)} %get-tuple-element.96.norm_gain, bf16[288,1536]{1,0:T(8,128)(2,1)S(1)} %get-tuple-element.103.x, ...), custom_call_target="tpu_custom_call" | custom-call | flops 2000000000 | bytes 8388608 | tf_op jit(solution)/shard_map/pallas_call | solution.py:435
  46.7 0.6 collective-permute-start.5
  47.3 0.0 collective-permute-done.19.b
  47.3 0.2 shard_map.179
  47.5 1.6 %collective-permute-start.20 = (bf16[2,16,32,256]{3,2,1,0:T(8,128)(2,1)S(1)}, bf16[2,16,32,256]{3,2,1,0:T(8,128)(2,1)S(1)}, u32[]{:S(2)}, u32[]{:S(2)}) collective-permute-start(bf16[2,16,32,256]{3,2,1,0:T(8,128)(2,1)S(1)} %get-tuple-element.147), channel_id=1, source_target_pairs={{0,32},{1,33},{2,34},{3,35},{4,36},{5,37},{6,38},{7,39},{8,40},{9,... | collective-permute-start | bytes 1572872 | tf_op jit(solution)/shard_map/ppermute | solution.py:484
  49.1 0.0 collective-permute-done.12.b
  49.1 0.2 shard_map.173
  49.3 1.8 %collective-permute-start.13 = (bf16[2,16,32,256]{3,2,1,0:T(8,128)(2,1)S(1)}, bf16[2,16,32,256]{3,2,1,0:T(8,128)(2,1)S(1)}, u32[]{:S(2)}, u32[]{:S(2)}) collective-permute-start(bf16[2,16,32,256]{3,2,1,0:T(8,128)(2,1)S(1)} %get-tuple-element.133), channel_id=1, source_target_pairs={{0,4},{1,5},{2,6},{3,7},{4,0},{5,1},{6,2},{7,3},{8,12},{9,13},{10,... | collective-permute-start | bytes 1572872 | tf_op jit(solution)/shard_map/ppermute | solution.py:484
  51.1 0.0 collective-permute-done.5.b
  51.1 0.2 shard_map.166
  51.3 0.1 collective-permute-start.6
  51.4 5.4 %collective-permute-done.20.got = bf16[2,16,32,256]{3,2,1,0:T(8,128)(2,1)S(1)} collective-permute-done((bf16[2,16,32,256]{3,2,1,0:T(8,128)(2,1)S(1)}, bf16[2,16,32,256]{3,2,1,0:T(8,128)(2,1)S(1)}, u32[]{:S(2)}, u32[]{:S(2)}) %collective-permute-start.20) | collective-permute-done | bytes 524320 | tf_op jit(solution)/shard_map/ppermute | solution.py:484
  56.7 0.1 shard_map.180
  56.8 2.6 %collective-permute-start.21 = (bf16[16,32,256]{2,1,0:T(8,128)(2,1)S(1)}, bf16[16,32,256]{2,1,0:T(8,128)(2,1)S(1)}, u32[]{:S(2)}, u32[]{:S(2)}) collective-permute-start(bf16[16,32,256]{2,1,0:T(8,128)(2,1)S(1)} %get-tuple-element.149), channel_id=1, source_target_pairs={{0,96},{1,97},{2,98},{3,99},{4,100},{5,101},{6,102},{7,103},{8,104... | collective-permute-start | bytes 786440 | tf_op jit(solution)/shard_map/ppermute | solution.py:484
  59.4 0.0 collective-permute-done.13.got
  59.4 0.1 shard_map.174
  59.5 2.2 %collective-permute-start.14 = (bf16[16,32,256]{2,1,0:T(8,128)(2,1)S(1)}, bf16[16,32,256]{2,1,0:T(8,128)(2,1)S(1)}, u32[]{:S(2)}, u32[]{:S(2)}) collective-permute-start(bf16[16,32,256]{2,1,0:T(8,128)(2,1)S(1)} %get-tuple-element.135), channel_id=1, source_target_pairs={{0,12},{1,13},{2,14},{3,15},{4,8},{5,9},{6,10},{7,11},{8,4},{9,5},... | collective-permute-start | bytes 786440 | tf_op jit(solution)/shard_map/ppermute | solution.py:484
  61.7 0.0 collective-permute-done.6.got
  61.7 0.1 shard_map.167
  61.7 1.2 %collective-permute-start.7 = (bf16[16,32,256]{2,1,0:T(8,128)(2,1)S(1)}, bf16[16,32,256]{2,1,0:T(8,128)(2,1)S(1)}, u32[]{:S(2)}, u32[]{:S(2)}) collective-permute-start(bf16[16,32,256]{2,1,0:T(8,128)(2,1)S(1)} %get-tuple-element.114), channel_id=1, source_target_pairs={{0,3},{1,2},{2,1},{3,0},{4,7},{5,6},{6,5},{7,4},{8,11},{9,10},{10,... | collective-permute-start | bytes 786440 | tf_op jit(solution)/shard_map/ppermute | solution.py:484
  62.9 1.5 %collective-permute-done.21.b = bf16[16,32,256]{2,1,0:T(8,128)(2,1)S(1)} collective-permute-done((bf16[16,32,256]{2,1,0:T(8,128)(2,1)S(1)}, bf16[16,32,256]{2,1,0:T(8,128)(2,1)S(1)}, u32[]{:S(2)}, u32[]{:S(2)}) %collective-permute-start.21) | collective-permute-done | bytes 262176 | tf_op jit(solution)/shard_map/ppermute | solution.py:484
  64.5 0.1 collective-permute-start.22
  64.6 2.5 %collective-permute-done.14.b = bf16[16,32,256]{2,1,0:T(8,128)(2,1)S(1)} collective-permute-done((bf16[16,32,256]{2,1,0:T(8,128)(2,1)S(1)}, bf16[16,32,256]{2,1,0:T(8,128)(2,1)S(1)}, u32[]{:S(2)}, u32[]{:S(2)}) %collective-permute-start.14) | collective-permute-done | bytes 262176 | tf_op jit(solution)/shard_map/ppermute | solution.py:484
  67.2 0.7 collective-permute-start.15
  67.9 2.8 %collective-permute-done.7.b = bf16[16,32,256]{2,1,0:T(8,128)(2,1)S(1)} collective-permute-done((bf16[16,32,256]{2,1,0:T(8,128)(2,1)S(1)}, bf16[16,32,256]{2,1,0:T(8,128)(2,1)S(1)}, u32[]{:S(2)}, u32[]{:S(2)}) %collective-permute-start.7) | collective-permute-done | bytes 262176 | tf_op jit(solution)/shard_map/ppermute | solution.py:484
  70.7 0.1 collective-permute-start.8
  70.8 1.0 %collective-permute-start.23 = (bf16[4,32,256]{2,1,0:T(8,128)(2,1)S(1)}, bf16[4,32,256]{2,1,0:T(8,128)(2,1)S(1)}, u32[]{:S(2)}, u32[]{:S(2)}) collective-permute-start(bf16[4,32,256]{2,1,0:T(8,128)(2,1)S(1)} %get-tuple-element.153), channel_id=1, source_target_pairs={{0,3},{1,2},{2,1},{3,0},{4,7},{5,6},{6,5},{7,4},{8,11},{9,10},{10,... | collective-permute-start | bytes 196616 | tf_op jit(solution)/shard_map/ppermute | solution.py:484
  71.8 0.4 collective-permute-done.15.got
  72.2 1.4 %collective-permute-start.16 = (bf16[4,32,256]{2,1,0:T(8,128)(2,1)S(1)}, bf16[4,32,256]{2,1,0:T(8,128)(2,1)S(1)}, u32[]{:S(2)}, u32[]{:S(2)}) collective-permute-start(bf16[4,32,256]{2,1,0:T(8,128)(2,1)S(1)} %get-tuple-element.139), channel_id=1, source_target_pairs={{0,96},{1,97},{2,98},{3,99},{4,100},{5,101},{6,102},{7,103},{8,104... | collective-permute-start | bytes 196616 | tf_op jit(solution)/shard_map/ppermute | solution.py:484
  73.6 2.1 %collective-permute-done.8.got = bf16[2,4,32,256]{3,2,1,0:T(8,128)(2,1)S(1)} collective-permute-done((bf16[2,4,32,256]{3,2,1,0:T(8,128)(2,1)S(1)}, bf16[2,4,32,256]{3,2,1,0:T(8,128)(2,1)S(1)}, u32[]{:S(2)}, u32[]{:S(2)}) %collective-permute-start.8) | collective-permute-done | bytes 131104 | tf_op jit(solution)/shard_map/ppermute | solution.py:484
  75.8 0.9 %collective-permute-start.9 = (bf16[4,32,256]{2,1,0:T(8,128)(2,1)S(1)}, bf16[4,32,256]{2,1,0:T(8,128)(2,1)S(1)}, u32[]{:S(2)}, u32[]{:S(2)}) collective-permute-start(bf16[4,32,256]{2,1,0:T(8,128)(2,1)S(1)} %get-tuple-element.118), channel_id=1, source_target_pairs={{0,12},{1,13},{2,14},{3,15},{4,8},{5,9},{6,10},{7,11},{8,4},{9,5},... | collective-permute-start | bytes 196616 | tf_op jit(solution)/shard_map/ppermute | solution.py:484
  76.7 0.0 collective-permute-done.23.b
  76.7 1.7 %collective-permute-start.24 = (bf16[2,1,32,256]{3,2,1,0:T(8,128)(2,1)S(1)}, bf16[2,1,32,256]{3,2,1,0:T(8,128)(2,1)S(1)}, u32[]{:S(2)}, u32[]{:S(2)}) collective-permute-start(bf16[2,1,32,256]{3,2,1,0:T(8,128)(2,1)S(1)} %get-tuple-element.155), channel_id=1, source_target_pairs={{0,4},{1,5},{2,6},{3,7},{4,0},{5,1},{6,2},{7,3},{8,12},{9,13},{10,... | collective-permute-start | bytes 98312 | tf_op jit(solution)/shard_map/ppermute | solution.py:484
  78.4 0.0 collective-permute-done.16.b
  78.4 0.1 collective-permute-start.17
  78.5 2.8 %collective-permute-done.9.b = bf16[4,32,256]{2,1,0:T(8,128)(2,1)S(1)} collective-permute-done((bf16[4,32,256]{2,1,0:T(8,128)(2,1)S(1)}, bf16[4,32,256]{2,1,0:T(8,128)(2,1)S(1)}, u32[]{:S(2)}, u32[]{:S(2)}) %collective-permute-start.9) | collective-permute-done | bytes 65568 | tf_op jit(solution)/shard_map/ppermute | solution.py:484
  81.3 1.3 %collective-permute-start.10 = (bf16[2,1,32,256]{3,2,1,0:T(8,128)(2,1)S(1)}, bf16[2,1,32,256]{3,2,1,0:T(8,128)(2,1)S(1)}, u32[]{:S(2)}, u32[]{:S(2)}) collective-permute-start(bf16[2,1,32,256]{3,2,1,0:T(8,128)(2,1)S(1)} %get-tuple-element.120), channel_id=1, source_target_pairs={{0,32},{1,33},{2,34},{3,35},{4,36},{5,37},{6,38},{7,39},{8,40},{9,... | collective-permute-start | bytes 98312 | tf_op jit(solution)/shard_map/ppermute | solution.py:484
  82.7 0.5 collective-permute-start.25
  83.2 0.0 collective-permute-done.17.got
  83.3 0.8 collective-permute-start.18
  84.1 1.3 %collective-permute-done.10.got = bf16[2,1,32,256]{3,2,1,0:T(8,128)(2,1)S(1)} collective-permute-done((bf16[2,1,32,256]{3,2,1,0:T(8,128)(2,1)S(1)}, bf16[2,1,32,256]{3,2,1,0:T(8,128)(2,1)S(1)}, u32[]{:S(2)}, u32[]{:S(2)}) %collective-permute-start.10) | collective-permute-done | bytes 32800 | tf_op jit(solution)/shard_map/ppermute | solution.py:484
  85.4 3.0 %collective-permute-start.11 = (bf16[1,32,256]{2,1,0:T(8,128)(2,1)S(1)}, bf16[1,32,256]{2,1,0:T(8,128)(2,1)S(1)}, u32[]{:S(2)}, u32[]{:S(2)}) collective-permute-start(bf16[1,32,256]{2,1,0:T(8,128)(2,1)S(1)} %get-tuple-element.122), channel_id=1, source_target_pairs={{0,96},{1,97},{2,98},{3,99},{4,100},{5,101},{6,102},{7,103},{8,104... | collective-permute-start | bytes 49160 | tf_op jit(solution)/shard_map/ppermute | solution.py:484
  88.4 0.0 collective-permute-done.25.refs_5_
  88.4 0.0 collective-permute-done.18.refs_3_
  88.4 1.9 %collective-permute-done.11.refs_1_ = bf16[1,32,256]{2,1,0:T(8,128)(2,1)S(1)} collective-permute-done((bf16[1,32,256]{2,1,0:T(8,128)(2,1)S(1)}, bf16[1,32,256]{2,1,0:T(8,128)(2,1)S(1)}, u32[]{:S(2)}, u32[]{:S(2)}) %collective-permute-start.11) | collective-permute-done | bytes 16416 | tf_op jit(solution)/shard_map/ppermute | solution.py:484
  90.3 0.7 shard_map.185
  (15 shorter events, 0.2 us)
Async XLA Ops:
  3.1 23.0 %all-to-all-start = ((bf16[64,8,256]{2,1,0:T(8,128)(2,1)}), bf16[64,8,256]{2,1,0:T(8,128)(2,1)S(1)}, u32[]{:S(2)}, u32[]{:S(2)}) async-start(bf16[64,8,256]{2,1,0:T(8,128)(2,1)} %get-tuple-element.87), calls=%async_computation | async-start | bytes 524288 | tf_op jit(solution)/shard_map/all_to_all | solution.py:579
  14.6 13.3 %collective-permute-start = (bf16[256,512]{1,0:T(8,128)(2,1)S(1)}, bf16[256,512]{1,0:T(8,128)(2,1)S(1)}, u32[]{:S(2)}, u32[]{:S(2)}) collective-permute-start(bf16[256,512]{1,0:T(8,128)(2,1)S(1)} %get-tuple-element.82), channel_id=1, source_target_pairs={{0,1},{1,2},{2,3},{3,4},{4,5},{5,6},{6,7},{7,8},{8,9},{9,10},{10,1... | collective-permute-start | bytes 786440 | tf_op jit(solution)/shard_map/ppermute | solution.py:577
  16.3 11.7 %collective-permute-start.1 = (bf16[256,512]{1,0:T(8,128)(2,1)S(1)}, bf16[256,512]{1,0:T(8,128)(2,1)S(1)}, u32[]{:S(2)}, u32[]{:S(2)}) collective-permute-start(bf16[256,512]{1,0:T(8,128)(2,1)S(1)} %get-tuple-element.83), channel_id=1, source_target_pairs={{0,15},{1,0},{2,1},{3,2},{4,3},{5,4},{6,5},{7,6},{8,7},{9,8},{10,9... | collective-permute-start | bytes 786440 | tf_op jit(solution)/shard_map/ppermute | solution.py:578
  26.1 2.7 %collective-permute-start.4 = (bf16[512,256]{1,0:T(8,128)(2,1)S(1)}, bf16[512,256]{1,0:T(8,128)(2,1)S(1)}, u32[]{:S(2)}, u32[]{:S(2)}) collective-permute-start(bf16[512,256]{1,0:T(8,128)(2,1)S(1)} %bitcast.3), channel_id=1, source_target_pairs={{0,16},{16,0},{1,17},{17,1},{2,18},{18,2},{3,19},{19,3},{4,20},{20... | collective-permute-start | bytes 786440 | tf_op jit(solution)/shard_map/ppermute | solution.py:584
  28.0 4.3 %collective-permute-start.2 = (bf16[256,512]{1,0:T(8,128)(2,1)S(1)}, bf16[256,512]{1,0:T(8,128)(2,1)S(1)}, u32[]{:S(2)}, u32[]{:S(2)}) collective-permute-start(bf16[256,512]{1,0:T(8,128)(2,1)S(1)} %get-tuple-element.85), channel_id=1, source_target_pairs={{0,16},{16,0},{1,17},{17,1},{2,18},{18,2},{3,19},{19,3},{4,20},{20... | collective-permute-start | bytes 786440 | tf_op jit(solution)/shard_map/ppermute | solution.py:583
  28.1 4.2 %collective-permute-start.3 = (bf16[256,512]{1,0:T(8,128)(2,1)S(1)}, bf16[256,512]{1,0:T(8,128)(2,1)S(1)}, u32[]{:S(2)}, u32[]{:S(2)}) collective-permute-start(bf16[256,512]{1,0:T(8,128)(2,1)S(1)} %get-tuple-element.86), channel_id=1, source_target_pairs={{16,32},{32,16},{17,33},{33,17},{18,34},{34,18},{19,35},{35,19},{2... | collective-permute-start | bytes 786440 | tf_op jit(solution)/shard_map/ppermute | solution.py:582
  38.0 9.3 %collective-permute-start.19 = (bf16[64,32,256]{2,1,0:T(8,128)(2,1)S(1)}, bf16[64,32,256]{2,1,0:T(8,128)(2,1)S(1)}, u32[]{:S(2)}, u32[]{:S(2)}) collective-permute-start(bf16[64,32,256]{2,1,0:T(8,128)(2,1)S(1)} %get-tuple-element.145), channel_id=1, source_target_pairs={{0,16},{16,0},{1,17},{17,1},{2,18},{18,2},{3,19},{19,3},{4,20},{20... | collective-permute-start | bytes 3145736 | tf_op jit(solution)/shard_map/ppermute | solution.py:621
  44.5 4.6 %collective-permute-start.12 = (bf16[64,32,256]{2,1,0:T(8,128)(2,1)S(1)}, bf16[64,32,256]{2,1,0:T(8,128)(2,1)S(1)}, u32[]{:S(2)}, u32[]{:S(2)}) collective-permute-start(bf16[64,32,256]{2,1,0:T(8,128)(2,1)S(1)} %get-tuple-element.131), channel_id=1, source_target_pairs={{0,16},{16,0},{1,17},{17,1},{2,18},{18,2},{3,19},{19,3},{4,20},{20... | collective-permute-start | bytes 3145736 | tf_op jit(solution)/shard_map/ppermute | solution.py:627
  46.7 4.4 %collective-permute-start.5 = (bf16[64,32,256]{2,1,0:T(8,128)(2,1)S(1)}, bf16[64,32,256]{2,1,0:T(8,128)(2,1)S(1)}, u32[]{:S(2)}, u32[]{:S(2)}) collective-permute-start(bf16[64,32,256]{2,1,0:T(8,128)(2,1)S(1)} %get-tuple-element.110), channel_id=1, source_target_pairs={{0,16},{16,0},{1,17},{17,1},{2,18},{18,2},{3,19},{19,3},{4,20},{20... | collective-permute-start | bytes 3145736 | tf_op jit(solution)/shard_map/ppermute | solution.py:627
  47.5 9.3 %collective-permute-start.20 = (bf16[2,16,32,256]{3,2,1,0:T(8,128)(2,1)S(1)}, bf16[2,16,32,256]{3,2,1,0:T(8,128)(2,1)S(1)}, u32[]{:S(2)}, u32[]{:S(2)}) collective-permute-start(bf16[2,16,32,256]{3,2,1,0:T(8,128)(2,1)S(1)} %get-tuple-element.147), channel_id=1, source_target_pairs={{0,32},{1,33},{2,34},{3,35},{4,36},{5,37},{6,38},{7,39},{8,40},{9,... | collective-permute-start | bytes 1572872 | tf_op jit(solution)/shard_map/ppermute | solution.py:484
  49.3 10.1 %collective-permute-start.13 = (bf16[2,16,32,256]{3,2,1,0:T(8,128)(2,1)S(1)}, bf16[2,16,32,256]{3,2,1,0:T(8,128)(2,1)S(1)}, u32[]{:S(2)}, u32[]{:S(2)}) collective-permute-start(bf16[2,16,32,256]{3,2,1,0:T(8,128)(2,1)S(1)} %get-tuple-element.133), channel_id=1, source_target_pairs={{0,4},{1,5},{2,6},{3,7},{4,0},{5,1},{6,2},{7,3},{8,12},{9,13},{10,... | collective-permute-start | bytes 1572872 | tf_op jit(solution)/shard_map/ppermute | solution.py:484
  51.3 10.4 %collective-permute-start.6 = (bf16[2,16,32,256]{3,2,1,0:T(8,128)(2,1)S(1)}, bf16[2,16,32,256]{3,2,1,0:T(8,128)(2,1)S(1)}, u32[]{:S(2)}, u32[]{:S(2)}) collective-permute-start(bf16[2,16,32,256]{3,2,1,0:T(8,128)(2,1)S(1)} %get-tuple-element.112), channel_id=1, source_target_pairs={{0,1},{1,0},{2,3},{3,2},{4,5},{5,4},{6,7},{7,6},{8,9},{9,8},{10,11... | collective-permute-start | bytes 1572872 | tf_op jit(solution)/shard_map/ppermute | solution.py:484
  56.8 7.7 %collective-permute-start.21 = (bf16[16,32,256]{2,1,0:T(8,128)(2,1)S(1)}, bf16[16,32,256]{2,1,0:T(8,128)(2,1)S(1)}, u32[]{:S(2)}, u32[]{:S(2)}) collective-permute-start(bf16[16,32,256]{2,1,0:T(8,128)(2,1)S(1)} %get-tuple-element.149), channel_id=1, source_target_pairs={{0,96},{1,97},{2,98},{3,99},{4,100},{5,101},{6,102},{7,103},{8,104... | collective-permute-start | bytes 786440 | tf_op jit(solution)/shard_map/ppermute | solution.py:484
  59.5 7.7 %collective-permute-start.14 = (bf16[16,32,256]{2,1,0:T(8,128)(2,1)S(1)}, bf16[16,32,256]{2,1,0:T(8,128)(2,1)S(1)}, u32[]{:S(2)}, u32[]{:S(2)}) collective-permute-start(bf16[16,32,256]{2,1,0:T(8,128)(2,1)S(1)} %get-tuple-element.135), channel_id=1, source_target_pairs={{0,12},{1,13},{2,14},{3,15},{4,8},{5,9},{6,10},{7,11},{8,4},{9,5},... | collective-permute-start | bytes 786440 | tf_op jit(solution)/shard_map/ppermute | solution.py:484
  61.7 8.9 %collective-permute-start.7 = (bf16[16,32,256]{2,1,0:T(8,128)(2,1)S(1)}, bf16[16,32,256]{2,1,0:T(8,128)(2,1)S(1)}, u32[]{:S(2)}, u32[]{:S(2)}) collective-permute-start(bf16[16,32,256]{2,1,0:T(8,128)(2,1)S(1)} %get-tuple-element.114), channel_id=1, source_target_pairs={{0,3},{1,2},{2,1},{3,0},{4,7},{5,6},{6,5},{7,4},{8,11},{9,10},{10,... | collective-permute-start | bytes 786440 | tf_op jit(solution)/shard_map/ppermute | solution.py:484
  64.5 6.3 %collective-permute-start.22 = (bf16[2,4,32,256]{3,2,1,0:T(8,128)(2,1)S(1)}, bf16[2,4,32,256]{3,2,1,0:T(8,128)(2,1)S(1)}, u32[]{:S(2)}, u32[]{:S(2)}) collective-permute-start(bf16[2,4,32,256]{3,2,1,0:T(8,128)(2,1)S(1)} %get-tuple-element.151), channel_id=1, source_target_pairs={{0,1},{1,0},{2,3},{3,2},{4,5},{5,4},{6,7},{7,6},{8,9},{9,8},{10,11... | collective-permute-start | bytes 393224 | tf_op jit(solution)/shard_map/ppermute | solution.py:484
  67.2 5.0 %collective-permute-start.15 = (bf16[2,4,32,256]{3,2,1,0:T(8,128)(2,1)S(1)}, bf16[2,4,32,256]{3,2,1,0:T(8,128)(2,1)S(1)}, u32[]{:S(2)}, u32[]{:S(2)}) collective-permute-start(bf16[2,4,32,256]{3,2,1,0:T(8,128)(2,1)S(1)} %get-tuple-element.137), channel_id=1, source_target_pairs={{0,32},{1,33},{2,34},{3,35},{4,36},{5,37},{6,38},{7,39},{8,40},{9,... | collective-permute-start | bytes 393224 | tf_op jit(solution)/shard_map/ppermute | solution.py:484
  70.7 5.1 %collective-permute-start.8 = (bf16[2,4,32,256]{3,2,1,0:T(8,128)(2,1)S(1)}, bf16[2,4,32,256]{3,2,1,0:T(8,128)(2,1)S(1)}, u32[]{:S(2)}, u32[]{:S(2)}) collective-permute-start(bf16[2,4,32,256]{3,2,1,0:T(8,128)(2,1)S(1)} %get-tuple-element.116), channel_id=1, source_target_pairs={{0,4},{1,5},{2,6},{3,7},{4,0},{5,1},{6,2},{7,3},{8,12},{9,13},{10,... | collective-permute-start | bytes 393224 | tf_op jit(solution)/shard_map/ppermute | solution.py:484
  70.8 5.9 %collective-permute-start.23 = (bf16[4,32,256]{2,1,0:T(8,128)(2,1)S(1)}, bf16[4,32,256]{2,1,0:T(8,128)(2,1)S(1)}, u32[]{:S(2)}, u32[]{:S(2)}) collective-permute-start(bf16[4,32,256]{2,1,0:T(8,128)(2,1)S(1)} %get-tuple-element.153), channel_id=1, source_target_pairs={{0,3},{1,2},{2,1},{3,0},{4,7},{5,6},{6,5},{7,4},{8,11},{9,10},{10,... | collective-permute-start | bytes 196616 | tf_op jit(solution)/shard_map/ppermute | solution.py:484
  72.2 6.2 %collective-permute-start.16 = (bf16[4,32,256]{2,1,0:T(8,128)(2,1)S(1)}, bf16[4,32,256]{2,1,0:T(8,128)(2,1)S(1)}, u32[]{:S(2)}, u32[]{:S(2)}) collective-permute-start(bf16[4,32,256]{2,1,0:T(8,128)(2,1)S(1)} %get-tuple-element.139), channel_id=1, source_target_pairs={{0,96},{1,97},{2,98},{3,99},{4,100},{5,101},{6,102},{7,103},{8,104... | collective-permute-start | bytes 196616 | tf_op jit(solution)/shard_map/ppermute | solution.py:484
  75.8 5.6 %collective-permute-start.9 = (bf16[4,32,256]{2,1,0:T(8,128)(2,1)S(1)}, bf16[4,32,256]{2,1,0:T(8,128)(2,1)S(1)}, u32[]{:S(2)}, u32[]{:S(2)}) collective-permute-start(bf16[4,32,256]{2,1,0:T(8,128)(2,1)S(1)} %get-tuple-element.118), channel_id=1, source_target_pairs={{0,12},{1,13},{2,14},{3,15},{4,8},{5,9},{6,10},{7,11},{8,4},{9,5},... | collective-permute-start | bytes 196616 | tf_op jit(solution)/shard_map/ppermute | solution.py:484
  76.7 6.0 %collective-permute-start.24 = (bf16[2,1,32,256]{3,2,1,0:T(8,128)(2,1)S(1)}, bf16[2,1,32,256]{3,2,1,0:T(8,128)(2,1)S(1)}, u32[]{:S(2)}, u32[]{:S(2)}) collective-permute-start(bf16[2,1,32,256]{3,2,1,0:T(8,128)(2,1)S(1)} %get-tuple-element.155), channel_id=1, source_target_pairs={{0,4},{1,5},{2,6},{3,7},{4,0},{5,1},{6,2},{7,3},{8,12},{9,13},{10,... | collective-permute-start | bytes 98312 | tf_op jit(solution)/shard_map/ppermute | solution.py:484
  78.4 4.8 %collective-permute-start.17 = (bf16[2,1,32,256]{3,2,1,0:T(8,128)(2,1)S(1)}, bf16[2,1,32,256]{3,2,1,0:T(8,128)(2,1)S(1)}, u32[]{:S(2)}, u32[]{:S(2)}) collective-permute-start(bf16[2,1,32,256]{3,2,1,0:T(8,128)(2,1)S(1)} %get-tuple-element.141), channel_id=1, source_target_pairs={{0,1},{1,0},{2,3},{3,2},{4,5},{5,4},{6,7},{7,6},{8,9},{9,8},{10,11... | collective-permute-start | bytes 98312 | tf_op jit(solution)/shard_map/ppermute | solution.py:484
  81.3 4.0 %collective-permute-start.10 = (bf16[2,1,32,256]{3,2,1,0:T(8,128)(2,1)S(1)}, bf16[2,1,32,256]{3,2,1,0:T(8,128)(2,1)S(1)}, u32[]{:S(2)}, u32[]{:S(2)}) collective-permute-start(bf16[2,1,32,256]{3,2,1,0:T(8,128)(2,1)S(1)} %get-tuple-element.120), channel_id=1, source_target_pairs={{0,32},{1,33},{2,34},{3,35},{4,36},{5,37},{6,38},{7,39},{8,40},{9,... | collective-permute-start | bytes 98312 | tf_op jit(solution)/shard_map/ppermute | solution.py:484
  82.7 5.7 %collective-permute-start.25 = (bf16[1,32,256]{2,1,0:T(8,128)(2,1)S(1)}, bf16[1,32,256]{2,1,0:T(8,128)(2,1)S(1)}, u32[]{:S(2)}, u32[]{:S(2)}) collective-permute-start(bf16[1,32,256]{2,1,0:T(8,128)(2,1)S(1)} %get-tuple-element.157), channel_id=1, source_target_pairs={{0,12},{1,13},{2,14},{3,15},{4,8},{5,9},{6,10},{7,11},{8,4},{9,5},... | collective-permute-start | bytes 49160 | tf_op jit(solution)/shard_map/ppermute | solution.py:484
  83.3 5.1 %collective-permute-start.18 = (bf16[1,32,256]{2,1,0:T(8,128)(2,1)S(1)}, bf16[1,32,256]{2,1,0:T(8,128)(2,1)S(1)}, u32[]{:S(2)}, u32[]{:S(2)}) collective-permute-start(bf16[1,32,256]{2,1,0:T(8,128)(2,1)S(1)} %get-tuple-element.143), channel_id=1, source_target_pairs={{0,3},{1,2},{2,1},{3,0},{4,7},{5,6},{6,5},{7,4},{8,11},{9,10},{10,... | collective-permute-start | bytes 49160 | tf_op jit(solution)/shard_map/ppermute | solution.py:484
  85.4 4.9 %collective-permute-start.11 = (bf16[1,32,256]{2,1,0:T(8,128)(2,1)S(1)}, bf16[1,32,256]{2,1,0:T(8,128)(2,1)S(1)}, u32[]{:S(2)}, u32[]{:S(2)}) collective-permute-start(bf16[1,32,256]{2,1,0:T(8,128)(2,1)S(1)} %get-tuple-element.122), channel_id=1, source_target_pairs={{0,96},{1,97},{2,98},{3,99},{4,100},{5,101},{6,102},{7,103},{8,104... | collective-permute-start | bytes 49160 | tf_op jit(solution)/shard_map/ppermute | solution.py:484
where the time goes:
time: 91.3 us; the launch traced here: 91.1 us
  starting transfers between devices  43.8 us (48%)
  waiting for transfers between devices  28.6 us (31%)
  Pallas kernels  17.7 us (19%)
    ppermute x18, starting transfers between devices, swap_along(): return lax.ppermute(value, ALL, partner_pairs(axis, second))  21.3 us
    ppermute x18, waiting for transfers between devices, swap_along(): return lax.ppermute(value, ALL, partner_pairs(axis, second))  20.7 us
    all_to_all x1, starting transfers between devices, shards(): coarse_own = lax.all_to_all(coarse, ('z', 'x', 'y'), 0, 0, tiled=True)  11.5 us
    all_to_all x1, waiting for transfers between devices, shards(): coarse_own = lax.all_to_all(coarse, ('z', 'x', 'y'), 0, 0, tiled=True)  6 us
    pallas_call x1, Pallas kernels, node_pass(): pl.pallas_call(nodes_kernel, out_shape=[jax.ShapeDtypeStruct((256, D), BF...  5.66 us
    pallas_call x2, Pallas kernels, edge_pass(): pl.pallas_call(kernel, out_shape=[jax.ShapeDtypeStruct(*CHUNKS)] * 2, in_...  4.42 us
    ppermute x1, starting transfers between devices, shards(): terms = {2: reduced(2, keep, lax.ppermute(send, 'c', swap))}  4 us
    ppermute x1, starting transfers between devices, shards(): from_east = lax.ppermute(west, ALL, lon_pairs(-1, lats, lons))  3.78 us
  transfers between devices with their start and end apart: 27, of which 11 were waited for; matrix products, arithmetic and copies ran while one was open for 0% of the time, Pallas kernels for 10%

commit v1 on v0

--- a/solution.py
+++ b/solution.py
@@ -198,7 +198,7 @@
 )
 
 
-def local_kernel(from_west, from_east, coarse_own, coarse_other, *refs):
+def local_kernel(from_west, from_east, *refs):
     n = len(LOADED)
     hbm, vmem = refs[:n], refs[n : 2 * n]
     middle, received, pre, sem, table = refs[2 * n :]
@@ -227,15 +227,9 @@
     table[n_nodes : n_nodes + BORDER, :] = from_west[3 * SLOT_ROWS :, :]
     table[n_nodes + BORDER :, :] = from_east[3 * SLOT_ROWS :, :]
     sender = to["mesh_sender"][...]
-    line = jnp.where(sender < n_nodes, sender, jnp.where(sender < n_nodes + 2 * BORDER, -1, sender - 2 * BORDER))
-    near = dot_tn(down_onehot(line, table.shape[0]), table[...])
-    line = coarse_line(sender)
-    halves = coarse_own.shape[0]
-    for half in range(2):
-        hot = down_onehot(line + half * K_COARSE, 2 * halves)
-        part = dot_tn(hot[:halves], coarse_own[...]) + dot_tn(hot[halves:], coarse_other[...])
-        columns = slice(256 * half, 256 * (half + 1))
-        middle[:, columns] = (near[:, columns] + part).astype(BF16)
+    late = sender - 2 * BORDER
+    line = jnp.where(sender < n_nodes, sender, jnp.where(late < n_nodes, -1, late))
+    middle[...] = dot_tn(down_onehot(line, table.shape[0]), table[...]).astype(BF16)
     received[...] = dot_tn(down_onehot(to["edge_receiver"][...], n_nodes), nodes[...]).astype(BF16)
     for name in ("w_first_1", "edges", "first_bias"):
         loads[name].wait()
@@ -295,6 +289,8 @@
     centre,
     from_core,
     from_chip,
+    coarse_own,
+    coarse_other,
     owner,
     edge_sender,
     edge_receiver,
@@ -353,9 +349,17 @@
     borders[0:BORDER, :] = lower[3 * SLOT_ROWS :, :]
     borders[BORDER:, :] = upper[3 * SLOT_ROWS :, :]
 
-    bordering = dot_tn(down_onehot(edge_sender[...] - n_nodes, 2 * BORDER), borders[...])
+    sender = edge_sender[...]
+    near = middle[...].astype(F32)
+    near = near + dot_tn(down_onehot(sender - n_nodes, 2 * BORDER), borders[...])
+    line = coarse_line(sender)
+    halves = coarse_own.shape[0]
+    for half in range(2):
+        hot = down_onehot(line + half * K_COARSE, 2 * halves)
+        part = dot_tn(hot[:halves], coarse_own[...]) + dot_tn(hot[halves:], coarse_other[...])
+        to = slice(D + 256 * half, D + 256 * (half + 1))
+        x_edge[:, to] = (near[:, 256 * half : 256 * (half + 1)] + part).astype(BF16)
     x_edge[:, 0:D] = edges[...]
-    x_edge[:, D : 2 * D] = (middle[...].astype(F32) + bordering).astype(BF16)
     x_edge[:, 2 * D :] = received[...]
     pre = pre_edge[...] + dot(x_edge[:, D : 2 * D], w_first[1, D : 2 * D, :])
     y_edge = forward(
@@ -583,7 +587,7 @@
     from_core = lax.ppermute(to_core, "c", swap)
     coarse_other = lax.ppermute(coarse_own, "c", swap)
     at = local(
-        (from_west, from_east, coarse_own, coarse_other),
+        (from_west, from_east),
         (
             mesh_receiver,
             mesh_sender,
@@ -604,6 +608,8 @@
         middle,
         from_core,
         from_chip,
+        coarse_own,
+        coarse_other,
         at["owner"],
         at["mesh_sender"],
         at["edge_receiver"],

time: 91.3 us -> 89.1 us (0.976)
  blocking collectives: 0 us -> 18.5 us
  starting transfers between devices: 43.8 us -> 33.3 us
  waiting for transfers between devices: 28.6 us -> 18.6 us
    all_to_all x0 -> x1, blocking collectives: none -> 18.5 us  [shards(): coarse_own = lax.all_to_all(coarse, ('z', 'x', 'y'), 0, 0, tiled=True)]
    all_to_all x1 -> x0, starting transfers between devices: 11.5 us -> none  [shards(): coarse_own = lax.all_to_all(coarse, ('z', 'x', 'y'), 0, 0, tiled=True)]
    all_to_all x1 -> x0, waiting for transfers between devices: 6 us -> none  [shards(): coarse_own = lax.all_to_all(coarse, ('z', 'x', 'y'), 0, 0, tiled=True)]
    ppermute x18, waiting for transfers between devices: 20.7 us -> 17.5 us  [swap_along(): return lax.ppermute(value, ALL, partner_pairs(axis, second))]
    ppermute x1, waiting for transfers between devices: 1.87 us -> 0.01 us  [shards(): from_west = lax.ppermute(east, ALL, lon_pairs(1, lats, lons))]
    ppermute x2, waiting for transfers between devices: 0.01 us -> 1.11 us  [shards(): terms[k] = reduced(k, keep, lax.ppermute(send, 'c', swap))]
  transfers between devices with their start and end apart: 27 -> 26, of which waited for: 11 -> 12; matrix products, arithmetic and copies ran while one was open for 0% -> 0% of each run, Pallas kernels for 10% -> 10%
where the time goes in v1:
time: 89.1 us; the launch traced here: 88.9 us
  starting transfers between devices  33.3 us (37%)
  waiting for transfers between devices  18.6 us (21%)
  blocking collectives  18.5 us (21%)
  Pallas kernels  17.8 us (20%)
    ppermute x18, starting transfers between devices, swap_along(): return lax.ppermute(value, ALL, partner_pairs(axis, second))  22.2 us
    all_to_all x1, blocking collectives, shards(): coarse_own = lax.all_to_all(coarse, ('z', 'x', 'y'), 0, 0, tiled=True)  18.5 us
    ppermute x18, waiting for transfers between devices, swap_along(): return lax.ppermute(value, ALL, partner_pairs(axis, second))  17.5 us
    pallas_call x1, Pallas kernels, node_pass(): pl.pallas_call(nodes_kernel, out_shape=[jax.ShapeDtypeStruct((256, D), BF...  6.19 us
    pallas_call x2, Pallas kernels, edge_pass(): pl.pallas_call(kernel, out_shape=[jax.ShapeDtypeStruct(*CHUNKS)] * 2, in_...  4.41 us
    ppermute x1, starting transfers between devices, shards(): from_east = lax.ppermute(west, ALL, lon_pairs(-1, lats, lons))  3.71 us
    ppermute x1, starting transfers between devices, shards(): terms = {2: reduced(2, keep, lax.ppermute(send, 'c', swap))}  3.54 us
    pallas_call x1, Pallas kernels, local(): pl.pallas_call(local_kernel, out_shape=[jax.ShapeDtypeStruct(a.shape, a.d...  3.52 us
  transfers between devices with their start and end apart: 26, of which 12 were waited for; matrix products, arithmetic and copies ran while one was open for 0% of the time, Pallas kernels for 10%

profile of v1, /device:TPU:0, one launch (start us, length us, event | category | flops | bytes accessed | tf_op | source)
XLA Modules:
  0.0 88.9 jit_solution(17526168020104550282)
XLA Ops:
  0.6 2.0 %pack.1 = (bf16[256,512]{1,0:T(8,128)(2,1)S(1)}, bf16[256,512]{1,0:T(8,128)(2,1)S(1)}, bf16[256,512]{1,0:T(8,128)(2,1)S(1)}, bf16[64,8,256]{2,1,0:T(8,128)(2,1)S(1)}) custom-call(bf16[1024,512]{1,0:T(8,128)(2,1)} %refs_0_.2, bf16[288,512]{1,0:T(8,128)(2,1)} %refs_1_.2, s32[288]{0:T(512)} %refs_2_.2, bf16[256,512]{1,0:T(8,128)(2,1)} %refs_2_.3), custom_call_target="tpu_custom_call" | custom-call | flops 301989888 | bytes 2097152 | tf_op jit(solution)/shard_map/pack/pallas_call | solution.py:106
  2.6 1.8 %collective-permute-start = (bf16[256,512]{1,0:T(8,128)(2,1)S(1)}, bf16[256,512]{1,0:T(8,128)(2,1)S(1)}, u32[]{:S(2)}, u32[]{:S(2)}) collective-permute-start(bf16[256,512]{1,0:T(8,128)(2,1)S(1)} %get-tuple-element.82), channel_id=1, source_target_pairs={{0,1},{1,2},{2,3},{3,4},{4,5},{5,6},{6,7},{7,8},{8,9},{9,10},{10,1... | collective-permute-start | bytes 786440 | tf_op jit(solution)/shard_map/ppermute | solution.py:581
  4.4 3.7 %collective-permute-start.1 = (bf16[256,512]{1,0:T(8,128)(2,1)S(1)}, bf16[256,512]{1,0:T(8,128)(2,1)S(1)}, u32[]{:S(2)}, u32[]{:S(2)}) collective-permute-start(bf16[256,512]{1,0:T(8,128)(2,1)S(1)} %get-tuple-element.83), channel_id=1, source_target_pairs={{0,15},{1,0},{2,1},{3,2},{4,3},{5,4},{6,5},{7,6},{8,7},{9,8},{10,9... | collective-permute-start | bytes 786440 | tf_op jit(solution)/shard_map/ppermute | solution.py:582
  8.1 18.5 %all_to_all.5 = bf16[64,8,256]{2,1,0:T(8,128)(2,1)S(1)} all-to-all(bf16[64,8,256]{2,1,0:T(8,128)(2,1)S(1)} %get-tuple-element.87), channel_id=1, replica_groups=mesh['z'=4,'c'=2,'x'=4,'y'=4] {'z','x','y'}, dimensions={0} | all-to-all | bytes 524288 | tf_op jit(solution)/shard_map/all_to_all | solution.py:583
  26.6 0.0 collective-permute-start.4
  26.6 0.0 collective-permute-done.from_west
  26.6 0.0 collective-permute-done.1.from_east
  26.6 0.6 collective-permute-start.2
  27.2 0.7 collective-permute-start.3
  27.9 3.5 %local.1 = (s32[512]{0:T(512)S(1)}, s32[512]{0:T(512)S(1)}, bf16[256,512]{1,0:T(8,128)(2,1)S(1)}, bf16[3,1536,512]{2,1,0:T(8,128)(2,1)S(1)}, bf16[512,512]{1,0:T...) custom-call(bf16[256,512]{1,0:T(8,128)(2,1)S(1)} %collective-permute, ...), custom_call_target="tpu_custom_call" | custom-call | flops 2000000000 | bytes 10485760 | tf_op jit(solution)/shard_map/local/pallas_call | solution.py:249
  31.4 0.0 collective-permute-done.4.coarse_other
  31.4 0.0 collective-permute-done.2.from_core
  31.4 0.0 collective-permute-done.3.from_chip
  31.4 6.2 %node_pass.1 = (bf16[256,512]{1,0:T(8,128)(2,1)}, bf16[512,512]{1,0:T(8,128)(2,1)}, bf16[64,32,256]{2,1,0:T(8,128)(2,1)S(1)}, bf16[64,32,256]{2,1,0:T(8,128)(2,1...) custom-call(bf16[256,512]{1,0:T(8,128)(2,1)S(1)} %collective-permute, ...), custom_call_target="tpu_custom_call" | custom-call | flops 4000000000 | bytes 20971520 | tf_op jit(solution)/shard_map/node_pass/pallas_call | solution.py:402
  37.6 3.5 %collective-permute-start.19 = (bf16[64,32,256]{2,1,0:T(8,128)(2,1)S(1)}, bf16[64,32,256]{2,1,0:T(8,128)(2,1)S(1)}, u32[]{:S(2)}, u32[]{:S(2)}) collective-permute-start(bf16[64,32,256]{2,1,0:T(8,128)(2,1)S(1)} %get-tuple-element.145), channel_id=1, source_target_pairs={{0,16},{16,0},{1,17},{17,1},{2,18},{18,2},{3,19},{19,3},{4,20},{20... | collective-permute-start | bytes 3145736 | tf_op jit(solution)/shard_map/ppermute | solution.py:627
  41.2 2.5 %shard_map.172 = (bf16[64,32,256]{2,1,0:T(8,128)(2,1)S(1)}, bf16[64,32,256]{2,1,0:T(8,128)(2,1)S(1)}) custom-call(s32[512]{0:T(512)S(1)} %get-tuple-element.90.edge_receiver.index, bf16[3,512,512]{2,1,0:T(8,128)(2,1)S(1)} %get-tuple-element.95.w_second, f32[3,512]{1,0:T(4,128)S(1)} %get-tuple-element.96.norm_gain, ...), custom_call_target="tpu_custom_call" | custom-call | flops 2000000000 | bytes 8388608 | tf_op jit(solution)/shard_map/pallas_call | solution.py:439
  43.6 0.3 collective-permute-start.12
  43.9 1.9 %shard_map.165 = (bf16[64,32,256]{2,1,0:T(8,128)(2,1)S(1)}, bf16[64,32,256]{2,1,0:T(8,128)(2,1)S(1)}) custom-call(s32[288]{0:T(512)S(1)} %get-tuple-element.88.owner.index, bf16[3,512,512]{2,1,0:T(8,128)(2,1)S(1)} %get-tuple-element.95.w_second, f32[3,512]{1,0:T(4,128)S(1)} %get-tuple-element.96.norm_gain, bf16[288,1536]{1,0:T(8,128)(2,1)S(1)} %get-tuple-element.103.x, ...), custom_call_target="tpu_custom_call" | custom-call | flops 2000000000 | bytes 8388608 | tf_op jit(solution)/shard_map/pallas_call | solution.py:439
  45.9 0.6 collective-permute-start.5
  46.4 0.0 collective-permute-done.19.b
  46.5 0.2 shard_map.179
  46.6 0.5 collective-permute-start.20
  47.2 0.0 collective-permute-done.12.b
  47.2 0.2 shard_map.173
  47.3 0.3 collective-permute-start.13
  47.6 1.1 %collective-permute-done.5.b = bf16[64,32,256]{2,1,0:T(8,128)(2,1)S(1)} collective-permute-done((bf16[64,32,256]{2,1,0:T(8,128)(2,1)S(1)}, bf16[64,32,256]{2,1,0:T(8,128)(2,1)S(1)}, u32[]{:S(2)}, u32[]{:S(2)}) %collective-permute-start.5) | collective-permute-done | bytes 1048608 | tf_op jit(solution)/shard_map/ppermute | solution.py:633
  48.7 0.2 shard_map.166
  48.9 0.7 collective-permute-start.6
  49.6 6.3 %collective-permute-done.20.got = bf16[2,16,32,256]{3,2,1,0:T(8,128)(2,1)S(1)} collective-permute-done((bf16[2,16,32,256]{3,2,1,0:T(8,128)(2,1)S(1)}, bf16[2,16,32,256]{3,2,1,0:T(8,128)(2,1)S(1)}, u32[]{:S(2)}, u32[]{:S(2)}) %collective-permute-start.20) | collective-permute-done | bytes 524320 | tf_op jit(solution)/shard_map/ppermute | solution.py:488
  55.9 0.1 shard_map.180
  56.0 0.9 collective-permute-start.21
  56.8 0.0 collective-permute-done.13.got
  56.8 0.1 shard_map.174
  56.9 1.1 %collective-permute-start.14 = (bf16[16,32,256]{2,1,0:T(8,128)(2,1)S(1)}, bf16[16,32,256]{2,1,0:T(8,128)(2,1)S(1)}, u32[]{:S(2)}, u32[]{:S(2)}) collective-permute-start(bf16[16,32,256]{2,1,0:T(8,128)(2,1)S(1)} %get-tuple-element.135), channel_id=1, source_target_pairs={{0,12},{1,13},{2,14},{3,15},{4,8},{5,9},{6,10},{7,11},{8,4},{9,5},... | collective-permute-start | bytes 786440 | tf_op jit(solution)/shard_map/ppermute | solution.py:488
  58.0 0.1 collective-permute-done.6.got
  58.2 0.1 shard_map.167
  58.2 1.5 %collective-permute-start.7 = (bf16[16,32,256]{2,1,0:T(8,128)(2,1)S(1)}, bf16[16,32,256]{2,1,0:T(8,128)(2,1)S(1)}, u32[]{:S(2)}, u32[]{:S(2)}) collective-permute-start(bf16[16,32,256]{2,1,0:T(8,128)(2,1)S(1)} %get-tuple-element.114), channel_id=1, source_target_pairs={{0,3},{1,2},{2,1},{3,0},{4,7},{5,6},{6,5},{7,4},{8,11},{9,10},{10,... | collective-permute-start | bytes 786440 | tf_op jit(solution)/shard_map/ppermute | solution.py:488
  59.8 3.9 %collective-permute-done.21.b = bf16[16,32,256]{2,1,0:T(8,128)(2,1)S(1)} collective-permute-done((bf16[16,32,256]{2,1,0:T(8,128)(2,1)S(1)}, bf16[16,32,256]{2,1,0:T(8,128)(2,1)S(1)}, u32[]{:S(2)}, u32[]{:S(2)}) %collective-permute-start.21) | collective-permute-done | bytes 262176 | tf_op jit(solution)/shard_map/ppermute | solution.py:488
  63.7 0.7 collective-permute-start.22
  64.4 0.2 collective-permute-done.14.b
  64.6 1.5 %collective-permute-start.15 = (bf16[2,4,32,256]{3,2,1,0:T(8,128)(2,1)S(1)}, bf16[2,4,32,256]{3,2,1,0:T(8,128)(2,1)S(1)}, u32[]{:S(2)}, u32[]{:S(2)}) collective-permute-start(bf16[2,4,32,256]{3,2,1,0:T(8,128)(2,1)S(1)} %get-tuple-element.137), channel_id=1, source_target_pairs={{0,32},{1,33},{2,34},{3,35},{4,36},{5,37},{6,38},{7,39},{8,40},{9,... | collective-permute-start | bytes 393224 | tf_op jit(solution)/shard_map/ppermute | solution.py:488
  66.1 0.1 collective-permute-done.7.b
  66.2 0.9 %collective-permute-start.8 = (bf16[2,4,32,256]{3,2,1,0:T(8,128)(2,1)S(1)}, bf16[2,4,32,256]{3,2,1,0:T(8,128)(2,1)S(1)}, u32[]{:S(2)}, u32[]{:S(2)}) collective-permute-start(bf16[2,4,32,256]{3,2,1,0:T(8,128)(2,1)S(1)} %get-tuple-element.116), channel_id=1, source_target_pairs={{0,4},{1,5},{2,6},{3,7},{4,0},{5,1},{6,2},{7,3},{8,12},{9,13},{10,... | collective-permute-start | bytes 393224 | tf_op jit(solution)/shard_map/ppermute | solution.py:488
  67.1 1.6 %collective-permute-done.22.got = bf16[2,4,32,256]{3,2,1,0:T(8,128)(2,1)S(1)} collective-permute-done((bf16[2,4,32,256]{3,2,1,0:T(8,128)(2,1)S(1)}, bf16[2,4,32,256]{3,2,1,0:T(8,128)(2,1)S(1)}, u32[]{:S(2)}, u32[]{:S(2)}) %collective-permute-start.22) | collective-permute-done | bytes 131104 | tf_op jit(solution)/shard_map/ppermute | solution.py:488
  68.7 0.9 collective-permute-start.23
  69.6 0.1 collective-permute-done.15.got
  69.7 2.5 %collective-permute-start.16 = (bf16[4,32,256]{2,1,0:T(8,128)(2,1)S(1)}, bf16[4,32,256]{2,1,0:T(8,128)(2,1)S(1)}, u32[]{:S(2)}, u32[]{:S(2)}) collective-permute-start(bf16[4,32,256]{2,1,0:T(8,128)(2,1)S(1)} %get-tuple-element.139), channel_id=1, source_target_pairs={{0,96},{1,97},{2,98},{3,99},{4,100},{5,101},{6,102},{7,103},{8,104... | collective-permute-start | bytes 196616 | tf_op jit(solution)/shard_map/ppermute | solution.py:488
  72.2 0.0 collective-permute-done.8.got
  72.2 2.9 %collective-permute-start.9 = (bf16[4,32,256]{2,1,0:T(8,128)(2,1)S(1)}, bf16[4,32,256]{2,1,0:T(8,128)(2,1)S(1)}, u32[]{:S(2)}, u32[]{:S(2)}) collective-permute-start(bf16[4,32,256]{2,1,0:T(8,128)(2,1)S(1)} %get-tuple-element.118), channel_id=1, source_target_pairs={{0,12},{1,13},{2,14},{3,15},{4,8},{5,9},{6,10},{7,11},{8,4},{9,5},... | collective-permute-start | bytes 196616 | tf_op jit(solution)/shard_map/ppermute | solution.py:488
  75.1 0.0 collective-permute-done.23.b
  75.1 0.1 collective-permute-start.24
  75.2 0.0 collective-permute-done.16.b
  75.2 1.3 %collective-permute-start.17 = (bf16[2,1,32,256]{3,2,1,0:T(8,128)(2,1)S(1)}, bf16[2,1,32,256]{3,2,1,0:T(8,128)(2,1)S(1)}, u32[]{:S(2)}, u32[]{:S(2)}) collective-permute-start(bf16[2,1,32,256]{3,2,1,0:T(8,128)(2,1)S(1)} %get-tuple-element.141), channel_id=1, source_target_pairs={{0,1},{1,0},{2,3},{3,2},{4,5},{5,4},{6,7},{7,6},{8,9},{9,8},{10,11... | collective-permute-start | bytes 98312 | tf_op jit(solution)/shard_map/ppermute | solution.py:488
  76.5 1.3 %collective-permute-done.9.b = bf16[4,32,256]{2,1,0:T(8,128)(2,1)S(1)} collective-permute-done((bf16[4,32,256]{2,1,0:T(8,128)(2,1)S(1)}, bf16[4,32,256]{2,1,0:T(8,128)(2,1)S(1)}, u32[]{:S(2)}, u32[]{:S(2)}) %collective-permute-start.9) | collective-permute-done | bytes 65568 | tf_op jit(solution)/shard_map/ppermute | solution.py:488
  77.8 1.2 %collective-permute-start.10 = (bf16[2,1,32,256]{3,2,1,0:T(8,128)(2,1)S(1)}, bf16[2,1,32,256]{3,2,1,0:T(8,128)(2,1)S(1)}, u32[]{:S(2)}, u32[]{:S(2)}) collective-permute-start(bf16[2,1,32,256]{3,2,1,0:T(8,128)(2,1)S(1)} %get-tuple-element.120), channel_id=1, source_target_pairs={{0,32},{1,33},{2,34},{3,35},{4,36},{5,37},{6,38},{7,39},{8,40},{9,... | collective-permute-start | bytes 98312 | tf_op jit(solution)/shard_map/ppermute | solution.py:488
  79.0 0.1 collective-permute-done.24.got
  79.1 2.7 %collective-permute-start.25 = (bf16[1,32,256]{2,1,0:T(8,128)(2,1)S(1)}, bf16[1,32,256]{2,1,0:T(8,128)(2,1)S(1)}, u32[]{:S(2)}, u32[]{:S(2)}) collective-permute-start(bf16[1,32,256]{2,1,0:T(8,128)(2,1)S(1)} %get-tuple-element.157), channel_id=1, source_target_pairs={{0,12},{1,13},{2,14},{3,15},{4,8},{5,9},{6,10},{7,11},{8,4},{9,5},... | collective-permute-start | bytes 49160 | tf_op jit(solution)/shard_map/ppermute | solution.py:488
  81.8 0.0 collective-permute-done.17.got
  81.8 1.3 %collective-permute-start.18 = (bf16[1,32,256]{2,1,0:T(8,128)(2,1)S(1)}, bf16[1,32,256]{2,1,0:T(8,128)(2,1)S(1)}, u32[]{:S(2)}, u32[]{:S(2)}) collective-permute-start(bf16[1,32,256]{2,1,0:T(8,128)(2,1)S(1)} %get-tuple-element.143), channel_id=1, source_target_pairs={{0,3},{1,2},{2,1},{3,0},{4,7},{5,6},{6,5},{7,4},{8,11},{9,10},{10,... | collective-permute-start | bytes 49160 | tf_op jit(solution)/shard_map/ppermute | solution.py:488
  83.1 0.0 collective-permute-done.10.got
  83.2 1.3 %collective-permute-start.11 = (bf16[1,32,256]{2,1,0:T(8,128)(2,1)S(1)}, bf16[1,32,256]{2,1,0:T(8,128)(2,1)S(1)}, u32[]{:S(2)}, u32[]{:S(2)}) collective-permute-start(bf16[1,32,256]{2,1,0:T(8,128)(2,1)S(1)} %get-tuple-element.122), channel_id=1, source_target_pairs={{0,96},{1,97},{2,98},{3,99},{4,100},{5,101},{6,102},{7,103},{8,104... | collective-permute-start | bytes 49160 | tf_op jit(solution)/shard_map/ppermute | solution.py:488
  84.4 2.4 %collective-permute-done.18.refs_3_ = bf16[1,32,256]{2,1,0:T(8,128)(2,1)S(1)} collective-permute-done((bf16[1,32,256]{2,1,0:T(8,128)(2,1)S(1)}, bf16[1,32,256]{2,1,0:T(8,128)(2,1)S(1)}, u32[]{:S(2)}, u32[]{:S(2)}) %collective-permute-start.18) | collective-permute-done | bytes 16416 | tf_op jit(solution)/shard_map/ppermute | solution.py:488
  86.8 1.3 %collective-permute-done.11.refs_1_ = bf16[1,32,256]{2,1,0:T(8,128)(2,1)S(1)} collective-permute-done((bf16[1,32,256]{2,1,0:T(8,128)(2,1)S(1)}, bf16[1,32,256]{2,1,0:T(8,128)(2,1)S(1)}, u32[]{:S(2)}, u32[]{:S(2)}) %collective-permute-start.11) | collective-permute-done | bytes 16416 | tf_op jit(solution)/shard_map/ppermute | solution.py:488
  88.2 0.7 shard_map.185
  (14 shorter events, 0.2 us)
Async XLA Ops:
  2.6 24.0 %collective-permute-start = (bf16[256,512]{1,0:T(8,128)(2,1)S(1)}, bf16[256,512]{1,0:T(8,128)(2,1)S(1)}, u32[]{:S(2)}, u32[]{:S(2)}) collective-permute-start(bf16[256,512]{1,0:T(8,128)(2,1)S(1)} %get-tuple-element.82), channel_id=1, source_target_pairs={{0,1},{1,2},{2,3},{3,4},{4,5},{5,6},{6,7},{7,8},{8,9},{9,10},{10,1... | collective-permute-start | bytes 786440 | tf_op jit(solution)/shard_map/ppermute | solution.py:581
  4.4 22.2 %collective-permute-start.1 = (bf16[256,512]{1,0:T(8,128)(2,1)S(1)}, bf16[256,512]{1,0:T(8,128)(2,1)S(1)}, u32[]{:S(2)}, u32[]{:S(2)}) collective-permute-start(bf16[256,512]{1,0:T(8,128)(2,1)S(1)} %get-tuple-element.83), channel_id=1, source_target_pairs={{0,15},{1,0},{2,1},{3,2},{4,3},{5,4},{6,5},{7,6},{8,7},{9,8},{10,9... | collective-permute-start | bytes 786440 | tf_op jit(solution)/shard_map/ppermute | solution.py:582
  26.6 4.8 %collective-permute-start.4 = (bf16[512,256]{1,0:T(8,128)(2,1)S(1)}, bf16[512,256]{1,0:T(8,128)(2,1)S(1)}, u32[]{:S(2)}, u32[]{:S(2)}) collective-permute-start(bf16[512,256]{1,0:T(8,128)(2,1)S(1)} %bitcast.3), channel_id=1, source_target_pairs={{0,16},{16,0},{1,17},{17,1},{2,18},{18,2},{3,19},{19,3},{4,20},{20... | collective-permute-start | bytes 786440 | tf_op jit(solution)/shard_map/ppermute | solution.py:588
  26.6 4.8 %collective-permute-start.2 = (bf16[256,512]{1,0:T(8,128)(2,1)S(1)}, bf16[256,512]{1,0:T(8,128)(2,1)S(1)}, u32[]{:S(2)}, u32[]{:S(2)}) collective-permute-start(bf16[256,512]{1,0:T(8,128)(2,1)S(1)} %get-tuple-element.85), channel_id=1, source_target_pairs={{0,16},{16,0},{1,17},{17,1},{2,18},{18,2},{3,19},{19,3},{4,20},{20... | collective-permute-start | bytes 786440 | tf_op jit(solution)/shard_map/ppermute | solution.py:587
  27.2 4.2 %collective-permute-start.3 = (bf16[256,512]{1,0:T(8,128)(2,1)S(1)}, bf16[256,512]{1,0:T(8,128)(2,1)S(1)}, u32[]{:S(2)}, u32[]{:S(2)}) collective-permute-start(bf16[256,512]{1,0:T(8,128)(2,1)S(1)} %get-tuple-element.86), channel_id=1, source_target_pairs={{16,32},{32,16},{17,33},{33,17},{18,34},{34,18},{19,35},{35,19},{2... | collective-permute-start | bytes 786440 | tf_op jit(solution)/shard_map/ppermute | solution.py:586
  37.6 8.8 %collective-permute-start.19 = (bf16[64,32,256]{2,1,0:T(8,128)(2,1)S(1)}, bf16[64,32,256]{2,1,0:T(8,128)(2,1)S(1)}, u32[]{:S(2)}, u32[]{:S(2)}) collective-permute-start(bf16[64,32,256]{2,1,0:T(8,128)(2,1)S(1)} %get-tuple-element.145), channel_id=1, source_target_pairs={{0,16},{16,0},{1,17},{17,1},{2,18},{18,2},{3,19},{19,3},{4,20},{20... | collective-permute-start | bytes 3145736 | tf_op jit(solution)/shard_map/ppermute | solution.py:627
  43.6 3.5 %collective-permute-start.12 = (bf16[64,32,256]{2,1,0:T(8,128)(2,1)S(1)}, bf16[64,32,256]{2,1,0:T(8,128)(2,1)S(1)}, u32[]{:S(2)}, u32[]{:S(2)}) collective-permute-start(bf16[64,32,256]{2,1,0:T(8,128)(2,1)S(1)} %get-tuple-element.131), channel_id=1, source_target_pairs={{0,16},{16,0},{1,17},{17,1},{2,18},{18,2},{3,19},{19,3},{4,20},{20... | collective-permute-start | bytes 3145736 | tf_op jit(solution)/shard_map/ppermute | solution.py:633
  45.9 2.9 %collective-permute-start.5 = (bf16[64,32,256]{2,1,0:T(8,128)(2,1)S(1)}, bf16[64,32,256]{2,1,0:T(8,128)(2,1)S(1)}, u32[]{:S(2)}, u32[]{:S(2)}) collective-permute-start(bf16[64,32,256]{2,1,0:T(8,128)(2,1)S(1)} %get-tuple-element.110), channel_id=1, source_target_pairs={{0,16},{16,0},{1,17},{17,1},{2,18},{18,2},{3,19},{19,3},{4,20},{20... | collective-permute-start | bytes 3145736 | tf_op jit(solution)/shard_map/ppermute | solution.py:633
  46.6 9.3 %collective-permute-start.20 = (bf16[2,16,32,256]{3,2,1,0:T(8,128)(2,1)S(1)}, bf16[2,16,32,256]{3,2,1,0:T(8,128)(2,1)S(1)}, u32[]{:S(2)}, u32[]{:S(2)}) collective-permute-start(bf16[2,16,32,256]{3,2,1,0:T(8,128)(2,1)S(1)} %get-tuple-element.147), channel_id=1, source_target_pairs={{0,32},{1,33},{2,34},{3,35},{4,36},{5,37},{6,38},{7,39},{8,40},{9,... | collective-permute-start | bytes 1572872 | tf_op jit(solution)/shard_map/ppermute | solution.py:488
  47.3 9.5 %collective-permute-start.13 = (bf16[2,16,32,256]{3,2,1,0:T(8,128)(2,1)S(1)}, bf16[2,16,32,256]{3,2,1,0:T(8,128)(2,1)S(1)}, u32[]{:S(2)}, u32[]{:S(2)}) collective-permute-start(bf16[2,16,32,256]{3,2,1,0:T(8,128)(2,1)S(1)} %get-tuple-element.133), channel_id=1, source_target_pairs={{0,4},{1,5},{2,6},{3,7},{4,0},{5,1},{6,2},{7,3},{8,12},{9,13},{10,... | collective-permute-start | bytes 1572872 | tf_op jit(solution)/shard_map/ppermute | solution.py:488
  48.9 9.3 %collective-permute-start.6 = (bf16[2,16,32,256]{3,2,1,0:T(8,128)(2,1)S(1)}, bf16[2,16,32,256]{3,2,1,0:T(8,128)(2,1)S(1)}, u32[]{:S(2)}, u32[]{:S(2)}) collective-permute-start(bf16[2,16,32,256]{3,2,1,0:T(8,128)(2,1)S(1)} %get-tuple-element.112), channel_id=1, source_target_pairs={{0,1},{1,0},{2,3},{3,2},{4,5},{5,4},{6,7},{7,6},{8,9},{9,8},{10,11... | collective-permute-start | bytes 1572872 | tf_op jit(solution)/shard_map/ppermute | solution.py:488
  56.0 7.7 %collective-permute-start.21 = (bf16[16,32,256]{2,1,0:T(8,128)(2,1)S(1)}, bf16[16,32,256]{2,1,0:T(8,128)(2,1)S(1)}, u32[]{:S(2)}, u32[]{:S(2)}) collective-permute-start(bf16[16,32,256]{2,1,0:T(8,128)(2,1)S(1)} %get-tuple-element.149), channel_id=1, source_target_pairs={{0,96},{1,97},{2,98},{3,99},{4,100},{5,101},{6,102},{7,103},{8,104... | collective-permute-start | bytes 786440 | tf_op jit(solution)/shard_map/ppermute | solution.py:488
  56.9 7.7 %collective-permute-start.14 = (bf16[16,32,256]{2,1,0:T(8,128)(2,1)S(1)}, bf16[16,32,256]{2,1,0:T(8,128)(2,1)S(1)}, u32[]{:S(2)}, u32[]{:S(2)}) collective-permute-start(bf16[16,32,256]{2,1,0:T(8,128)(2,1)S(1)} %get-tuple-element.135), channel_id=1, source_target_pairs={{0,12},{1,13},{2,14},{3,15},{4,8},{5,9},{6,10},{7,11},{8,4},{9,5},... | collective-permute-start | bytes 786440 | tf_op jit(solution)/shard_map/ppermute | solution.py:488
  58.2 8.0 %collective-permute-start.7 = (bf16[16,32,256]{2,1,0:T(8,128)(2,1)S(1)}, bf16[16,32,256]{2,1,0:T(8,128)(2,1)S(1)}, u32[]{:S(2)}, u32[]{:S(2)}) collective-permute-start(bf16[16,32,256]{2,1,0:T(8,128)(2,1)S(1)} %get-tuple-element.114), channel_id=1, source_target_pairs={{0,3},{1,2},{2,1},{3,0},{4,7},{5,6},{6,5},{7,4},{8,11},{9,10},{10,... | collective-permute-start | bytes 786440 | tf_op jit(solution)/shard_map/ppermute | solution.py:488
  63.7 5.0 %collective-permute-start.22 = (bf16[2,4,32,256]{3,2,1,0:T(8,128)(2,1)S(1)}, bf16[2,4,32,256]{3,2,1,0:T(8,128)(2,1)S(1)}, u32[]{:S(2)}, u32[]{:S(2)}) collective-permute-start(bf16[2,4,32,256]{3,2,1,0:T(8,128)(2,1)S(1)} %get-tuple-element.151), channel_id=1, source_target_pairs={{0,1},{1,0},{2,3},{3,2},{4,5},{5,4},{6,7},{7,6},{8,9},{9,8},{10,11... | collective-permute-start | bytes 393224 | tf_op jit(solution)/shard_map/ppermute | solution.py:488
  64.6 5.0 %collective-permute-start.15 = (bf16[2,4,32,256]{3,2,1,0:T(8,128)(2,1)S(1)}, bf16[2,4,32,256]{3,2,1,0:T(8,128)(2,1)S(1)}, u32[]{:S(2)}, u32[]{:S(2)}) collective-permute-start(bf16[2,4,32,256]{3,2,1,0:T(8,128)(2,1)S(1)} %get-tuple-element.137), channel_id=1, source_target_pairs={{0,32},{1,33},{2,34},{3,35},{4,36},{5,37},{6,38},{7,39},{8,40},{9,... | collective-permute-start | bytes 393224 | tf_op jit(solution)/shard_map/ppermute | solution.py:488
  66.2 6.0 %collective-permute-start.8 = (bf16[2,4,32,256]{3,2,1,0:T(8,128)(2,1)S(1)}, bf16[2,4,32,256]{3,2,1,0:T(8,128)(2,1)S(1)}, u32[]{:S(2)}, u32[]{:S(2)}) collective-permute-start(bf16[2,4,32,256]{3,2,1,0:T(8,128)(2,1)S(1)} %get-tuple-element.116), channel_id=1, source_target_pairs={{0,4},{1,5},{2,6},{3,7},{4,0},{5,1},{6,2},{7,3},{8,12},{9,13},{10,... | collective-permute-start | bytes 393224 | tf_op jit(solution)/shard_map/ppermute | solution.py:488
  68.7 6.4 %collective-permute-start.23 = (bf16[4,32,256]{2,1,0:T(8,128)(2,1)S(1)}, bf16[4,32,256]{2,1,0:T(8,128)(2,1)S(1)}, u32[]{:S(2)}, u32[]{:S(2)}) collective-permute-start(bf16[4,32,256]{2,1,0:T(8,128)(2,1)S(1)} %get-tuple-element.153), channel_id=1, source_target_pairs={{0,3},{1,2},{2,1},{3,0},{4,7},{5,6},{6,5},{7,4},{8,11},{9,10},{10,... | collective-permute-start | bytes 196616 | tf_op jit(solution)/shard_map/ppermute | solution.py:488
  69.7 5.6 %collective-permute-start.16 = (bf16[4,32,256]{2,1,0:T(8,128)(2,1)S(1)}, bf16[4,32,256]{2,1,0:T(8,128)(2,1)S(1)}, u32[]{:S(2)}, u32[]{:S(2)}) collective-permute-start(bf16[4,32,256]{2,1,0:T(8,128)(2,1)S(1)} %get-tuple-element.139), channel_id=1, source_target_pairs={{0,96},{1,97},{2,98},{3,99},{4,100},{5,101},{6,102},{7,103},{8,104... | collective-permute-start | bytes 196616 | tf_op jit(solution)/shard_map/ppermute | solution.py:488
  72.2 5.6 %collective-permute-start.9 = (bf16[4,32,256]{2,1,0:T(8,128)(2,1)S(1)}, bf16[4,32,256]{2,1,0:T(8,128)(2,1)S(1)}, u32[]{:S(2)}, u32[]{:S(2)}) collective-permute-start(bf16[4,32,256]{2,1,0:T(8,128)(2,1)S(1)} %get-tuple-element.118), channel_id=1, source_target_pairs={{0,12},{1,13},{2,14},{3,15},{4,8},{5,9},{6,10},{7,11},{8,4},{9,5},... | collective-permute-start | bytes 196616 | tf_op jit(solution)/shard_map/ppermute | solution.py:488
  75.1 4.0 %collective-permute-start.24 = (bf16[2,1,32,256]{3,2,1,0:T(8,128)(2,1)S(1)}, bf16[2,1,32,256]{3,2,1,0:T(8,128)(2,1)S(1)}, u32[]{:S(2)}, u32[]{:S(2)}) collective-permute-start(bf16[2,1,32,256]{3,2,1,0:T(8,128)(2,1)S(1)} %get-tuple-element.155), channel_id=1, source_target_pairs={{0,4},{1,5},{2,6},{3,7},{4,0},{5,1},{6,2},{7,3},{8,12},{9,13},{10,... | collective-permute-start | bytes 98312 | tf_op jit(solution)/shard_map/ppermute | solution.py:488
  75.2 6.6 %collective-permute-start.17 = (bf16[2,1,32,256]{3,2,1,0:T(8,128)(2,1)S(1)}, bf16[2,1,32,256]{3,2,1,0:T(8,128)(2,1)S(1)}, u32[]{:S(2)}, u32[]{:S(2)}) collective-permute-start(bf16[2,1,32,256]{3,2,1,0:T(8,128)(2,1)S(1)} %get-tuple-element.141), channel_id=1, source_target_pairs={{0,1},{1,0},{2,3},{3,2},{4,5},{5,4},{6,7},{7,6},{8,9},{9,8},{10,11... | collective-permute-start | bytes 98312 | tf_op jit(solution)/shard_map/ppermute | solution.py:488
  77.8 5.3 %collective-permute-start.10 = (bf16[2,1,32,256]{3,2,1,0:T(8,128)(2,1)S(1)}, bf16[2,1,32,256]{3,2,1,0:T(8,128)(2,1)S(1)}, u32[]{:S(2)}, u32[]{:S(2)}) collective-permute-start(bf16[2,1,32,256]{3,2,1,0:T(8,128)(2,1)S(1)} %get-tuple-element.120), channel_id=1, source_target_pairs={{0,32},{1,33},{2,34},{3,35},{4,36},{5,37},{6,38},{7,39},{8,40},{9,... | collective-permute-start | bytes 98312 | tf_op jit(solution)/shard_map/ppermute | solution.py:488
  79.1 5.3 %collective-permute-start.25 = (bf16[1,32,256]{2,1,0:T(8,128)(2,1)S(1)}, bf16[1,32,256]{2,1,0:T(8,128)(2,1)S(1)}, u32[]{:S(2)}, u32[]{:S(2)}) collective-permute-start(bf16[1,32,256]{2,1,0:T(8,128)(2,1)S(1)} %get-tuple-element.157), channel_id=1, source_target_pairs={{0,12},{1,13},{2,14},{3,15},{4,8},{5,9},{6,10},{7,11},{8,4},{9,5},... | collective-permute-start | bytes 49160 | tf_op jit(solution)/shard_map/ppermute | solution.py:488
  81.8 5.0 %collective-permute-start.18 = (bf16[1,32,256]{2,1,0:T(8,128)(2,1)S(1)}, bf16[1,32,256]{2,1,0:T(8,128)(2,1)S(1)}, u32[]{:S(2)}, u32[]{:S(2)}) collective-permute-start(bf16[1,32,256]{2,1,0:T(8,128)(2,1)S(1)} %get-tuple-element.143), channel_id=1, source_target_pairs={{0,3},{1,2},{2,1},{3,0},{4,7},{5,6},{6,5},{7,4},{8,11},{9,10},{10,... | collective-permute-start | bytes 49160 | tf_op jit(solution)/shard_map/ppermute | solution.py:488
  83.2 5.0 %collective-permute-start.11 = (bf16[1,32,256]{2,1,0:T(8,128)(2,1)S(1)}, bf16[1,32,256]{2,1,0:T(8,128)(2,1)S(1)}, u32[]{:S(2)}, u32[]{:S(2)}) collective-permute-start(bf16[1,32,256]{2,1,0:T(8,128)(2,1)S(1)} %get-tuple-element.122), channel_id=1, source_target_pairs={{0,96},{1,97},{2,98},{3,99},{4,100},{5,101},{6,102},{7,103},{8,104... | collective-permute-start | bytes 49160 | tf_op jit(solution)/shard_map/ppermute | solution.py:488
